TPU v7x, 768 devices: a whole 4x8x12 slice. The times are simulated.
768 devices in a mesh: wide: 96 (over z, x, core), tile: 8 (over y).
Axes of the slice: x: 4, y: 8, z: 12, core: 2. Of those that a mesh axis runs over, the one named last changes fastest.
Arguments:
- interface_gaps: float32 [96, 8, 2, 192, 256], P('wide', 'tile'), may hold values from -50 to 50
- flexibility: bfloat16 [96, 8, 768, 768], P('wide', 'tile'), may hold values from -1 to 2, as said below
- dirichlet_schur: bfloat16 [96, 8, 768, 768], P('wide', 'tile'), may hold values from -1 to 2, as said below
- face_rows: int32 [96, 8, 4], P('wide', 'tile'), may hold values from 0 to 192, as said below
Outputs:
- multipliers: float32 [96, 8, 2, 192, 256], P('wide', 'tile')
- residual: float32 [96, 8, 2, 192, 256], P('wide', 'tile')
Inputs may be any that keep to these rules, and one draw needn't show every extreme that they name: `face_rows`: A subdomain's previous-face counts equal its neighbour's next-face counts; faces on the boundary of the grid have 0 rows, every other face 192 // 2 rows or more; some face has exactly 192 rows. `flexibility`: each subdomain's matrix is symmetric positive definite. `dirichlet_schur`: each subdomain's matrix is symmetric positive definite.
All inputs are finite; a program needn't handle non-finite values.
Results may differ from a plain program's by a relative error of at most 0.009.
The roundings to bfloat16 on the way count: a program that leaves them out, or rounds other values in their place, can miss the bound.
Values may be sent and summed in bfloat16 or wider, within the bound.
No kernel may reach another device: no remote copies, remote signals or barrier semaphores. Data moves between devices by JAX's collectives and lax.ppermute only.
A program may use at most 32 MiB of HBM per device.

v0:
```python
import jax
import jax.numpy as jnp
from jax import lax
from jax.sharding import PartitionSpec as P

ITERS = 3


def shifted(block, axis, distance):
    devices = range(lax.axis_size(axis))
    route = [(i - distance, i) for i in devices if i - distance in devices]
    return lax.ppermute(block, axis, route)


def owned_apply(matrix, owned_vec, face_mask):
    face_len, load_count = (owned_vec.shape[1], owned_vec.shape[2])
    owned_low = owned_vec.astype(jnp.bfloat16)
    below_wide = shifted(owned_low[0], "wide", 1)
    below_tile = shifted(owned_low[1], "tile", 1)
    lifted = jnp.concatenate([owned_low, -below_wide[None], -below_tile[None]], 0).reshape(
        4 * face_len, load_count
    )
    result = jnp.dot(matrix, lifted, preferred_element_type=jnp.float32).reshape(
        4, face_len, load_count
    )
    above_wide = shifted(result[2], "wide", -1)
    above_tile = shifted(result[3], "tile", -1)
    return jnp.stack([result[0] - above_wide, result[1] - above_tile]) * face_mask[:2]


def column_sums(residual, precond, mapped):
    gamma_part = jnp.sum(residual * precond, axis=(0, 1))
    curve_part = jnp.sum(precond * mapped, axis=(0, 1))
    return lax.psum((gamma_part, curve_part), ("wide", "tile"))


def per_device(interface_gaps, flexibility, dirichlet_schur, face_rows):
    face_len = interface_gaps.shape[3]
    counts = face_rows[0, 0]
    row_index = lax.broadcasted_iota(jnp.int32, (4, face_len, 1), 1)
    face_mask = (row_index < counts[:, None, None]).astype(jnp.float32)
    flex_mat = flexibility[0, 0]
    schur_mat = dirichlet_schur[0, 0]
    owned_gaps = interface_gaps[0, 0] * face_mask[:2]

    def operate(matrix, vector):
        return owned_apply(matrix, vector, face_mask)

    residual = owned_gaps
    multipliers = jnp.zeros_like(residual)
    precond = operate(schur_mat, residual)
    mapped = operate(flex_mat, precond)
    gamma_now, curvature = column_sums(residual, precond, mapped)
    step_len = gamma_now / curvature
    direction = precond
    along_dir = mapped
    for iteration in range(ITERS):
        multipliers = multipliers + step_len * direction
        residual = residual - step_len * along_dir
        if iteration + 1 < ITERS:
            precond = operate(schur_mat, residual)
            mapped = operate(flex_mat, precond)
            gamma_next, curvature = column_sums(residual, precond, mapped)
            scaling = gamma_next / gamma_now
            step_len = gamma_next / (curvature - scaling * gamma_next / step_len)
            direction = precond + scaling * direction
            along_dir = mapped + scaling * along_dir
            gamma_now = gamma_next
    return (multipliers[None, None], residual[None, None])


def solution(mesh):
    placed = (
        P("wide", "tile", None, None, None),
        P("wide", "tile", None, None),
        P("wide", "tile", None, None),
        P("wide", "tile", None),
    )
    return jax.shard_map(
        per_device,
        mesh=mesh,
        in_specs=placed,
        out_specs=(P("wide", "tile", None, None, None), P("wide", "tile", None, None, None)),
        check_vma=False,
    )
```

profile of v0, /device:TPU:33, one launch (start us, length us, event | category | flops | bytes accessed | tf_op | source)
XLA Modules:
  0.0 511.9 jit_solution(1082293458610828831)
XLA Ops:
  2.7 3.7 collective-permute-start
  6.4 2.3 collective-permute-start.1
  8.8 5.2 %collective-permute-done.1 = bf16[192,256]{0,1:T(8,128)(2,1)S(1)} collective-permute-done((bf16[192,256]{0,1:T(8,128)(2,1)S(1)}, bf16[192,256]{0,1:T(8,128)(2,1)S(1)}, u32[]{:S(2)}, u32[]{:S(2)}) %collective-permute-start.1) | collective-permute-done | bytes 98336 | tf_op jit(solution)/shard_map/ppermute | solution.py:12
  15.0 1.9 collective-permute-start.2
  16.9 1.9 collective-permute-start.3
  18.8 4.1 collective-permute-done.2
  23.0 3.6 collective-permute-done.3
  27.5 4.2 collective-permute-start.4
  31.7 1.9 collective-permute-start.5
  33.7 5.0 collective-permute-done.5
  41.5 2.1 collective-permute-start.6
  43.6 2.2 collective-permute-start.7
  45.7 3.9 collective-permute-done.6
  49.6 3.1 collective-permute-done.7
  53.9 117.6 %all-reduce.2 = (f32[256]{0:T(256)S(1)}, f32[256]{0:T(256)S(1)}) all-reduce(f32[256]{0:T(256)S(1)} %get-tuple-element.11, f32[256]{0:T(256)S(1)} %get-tuple-element.10), channel_id=1, replica_groups=mesh['wide'=96,'tile'=8] {'wide','tile'}, use_global_device_ids=true, to_apply=%region_1.0 | all-reduce | flops 512 | bytes 4096 | tf_op jit(solution)/shard_map/psum | solution.py:34
  171.6 4.2 collective-permute-start.8
  175.9 1.9 collective-permute-start.9
  177.8 5.0 collective-permute-done.9
  183.8 2.0 copy.13
  187.4 1.9 collective-permute-start.10
  189.4 1.9 collective-permute-start.11
  191.3 4.1 collective-permute-done.10
  195.4 3.1 collective-permute-done.11
  200.2 4.8 collective-permute-start.12
  205.0 1.9 collective-permute-start.13
  206.9 5.0 collective-permute-done.13
  212.8 2.0 copy.14
  216.5 2.1 collective-permute-start.14
  218.5 1.9 collective-permute-start.15
  220.5 4.1 collective-permute-done.14
  224.6 2.5 collective-permute-done.15
  228.8 108.1 %all-reduce.1 = (f32[256]{0:T(256)S(1)}, f32[256]{0:T(256)S(1)}) all-reduce(f32[256]{0:T(256)S(1)} %get-tuple-element.9, f32[256]{0:T(256)S(1)} %get-tuple-element.8), channel_id=1, replica_groups=mesh['wide'=96,'tile'=8] {'wide','tile'}, use_global_device_ids=true, to_apply=%region_5.0 | all-reduce | flops 512 | bytes 4096 | tf_op jit(solution)/shard_map/psum | solution.py:34
  336.9 2.1 fusion.46
  339.0 2.2 collective-permute-start.16
  341.2 1.9 collective-permute-start.17
  343.1 6.0 %collective-permute-done.17 = bf16[192,256]{0,1:T(8,128)(2,1)S(1)} collective-permute-done((bf16[192,256]{0,1:T(8,128)(2,1)S(1)}, bf16[192,256]{0,1:T(8,128)(2,1)S(1)}, u32[]{:S(2)}, u32[]{:S(2)}) %collective-permute-start.17) | collective-permute-done | bytes 98336 | tf_op jit(solution)/shard_map/ppermute | solution.py:12
  351.8 3.0 collective-permute-start.18
  354.7 4.7 collective-permute-done.18
  362.1 5.3 %collective-permute-done.19 = f32[192,256]{0,1:T(8,128)S(1)} collective-permute-done((f32[192,256]{0,1:T(8,128)S(1)}, f32[192,256]{0,1:T(8,128)S(1)}, u32[]{:S(2)}, u32[]{:S(2)}) %collective-permute-start.19) | collective-permute-done | bytes 196640 | tf_op jit(solution)/shard_map/ppermute | solution.py:12
  368.3 4.9 collective-permute-start.20
  373.2 1.9 collective-permute-start.21
  375.2 5.0 collective-permute-done.21
  381.1 2.0 copy.16
  384.8 2.1 collective-permute-start.22
  386.8 1.9 collective-permute-start.23
  388.7 5.0 collective-permute-done.22
  396.4 111.2 %all-reduce = (f32[256]{0:T(256)S(1)}, f32[256]{0:T(256)S(1)}) all-reduce(f32[256]{0:T(256)S(1)} %get-tuple-element.7, f32[256]{0:T(256)S(1)} %get-tuple-element.6), channel_id=1, replica_groups=mesh['wide'=96,'tile'=8] {'wide','tile'}, use_global_device_ids=true, to_apply=%region_9.0 | all-reduce | flops 512 | bytes 4096 | tf_op jit(solution)/shard_map/psum | solution.py:34
  507.6 2.4 fusion.15
  (95 shorter events, 30.0 us)
Async XLA Ops:
  0.6 13.7 %copy-start = (bf16[1,1,768,768]{3,2,1,0:T(8,128)(2,1)S(1)}, bf16[1,1,768,768]{3,2,1,0:T(8,128)(2,1)}, u32[]{:S(2)}) copy-start(bf16[1,1,768,768]{3,2,1,0:T(8,128)(2,1)} %param.6) | copy-start | bytes 3538948
  2.7 6.0 %collective-permute-start = (bf16[192,256]{0,1:T(8,128)(2,1)S(1)}, bf16[192,256]{0,1:T(8,128)(2,1)S(1)}, u32[]{:S(2)}, u32[]{:S(2)}) collective-permute-start(bf16[192,256]{0,1:T(8,128)(2,1)S(1)} %get-tuple-element.80), channel_id=1, source_target_pairs={{0,8},{8,16},{16,24},{24,32},{32,40},{40,48},{48,56},{56,64},{64,7... | collective-permute-start | bytes 294920 | tf_op jit(solution)/shard_map/ppermute | solution.py:12
  6.4 7.5 %collective-permute-start.1 = (bf16[192,256]{0,1:T(8,128)(2,1)S(1)}, bf16[192,256]{0,1:T(8,128)(2,1)S(1)}, u32[]{:S(2)}, u32[]{:S(2)}) collective-permute-start(bf16[192,256]{0,1:T(8,128)(2,1)S(1)} %get-tuple-element.81), channel_id=1, source_target_pairs={{0,1},{1,2},{2,3},{3,4},{4,5},{5,6},{6,7},{8,9},{9,10},{10,11},{11... | collective-permute-start | bytes 294920 | tf_op jit(solution)/shard_map/ppermute | solution.py:12
  15.0 8.0 %collective-permute-start.2 = (f32[192,256]{0,1:T(8,128)S(1)}, f32[192,256]{0,1:T(8,128)S(1)}, u32[]{:S(2)}, u32[]{:S(2)}) collective-permute-start(f32[192,256]{0,1:T(8,128)S(1)} %get-tuple-element.68), channel_id=1, source_target_pairs={{8,0},{16,8},{24,16},{32,24},{40,32},{48,40},{56,48},{64,56},{72,6... | collective-permute-start | bytes 589832 | tf_op jit(solution)/shard_map/ppermute | solution.py:12
  16.9 9.7 %collective-permute-start.3 = (f32[192,256]{0,1:T(8,128)S(1)}, f32[192,256]{0,1:T(8,128)S(1)}, u32[]{:S(2)}, u32[]{:S(2)}) collective-permute-start(f32[192,256]{0,1:T(8,128)S(1)} %get-tuple-element.69), channel_id=1, source_target_pairs={{1,0},{2,1},{3,2},{4,3},{5,4},{6,5},{7,6},{9,8},{10,9},{11,10},{12... | collective-permute-start | bytes 589832 | tf_op jit(solution)/shard_map/ppermute | solution.py:12
  27.5 6.2 %copy-start.2 = (f32[1,192,256]{1,2,0:T(8,128)}, f32[1,192,256]{1,2,0:T(8,128)S(1)}, u32[]{:S(2)}) copy-start(f32[1,192,256]{1,2,0:T(8,128)S(1)} %get-tuple-element.42) | copy-start | bytes 589828
  27.5 6.2 %copy-start.4 = (f32[1,192,256]{1,2,0:T(8,128)}, f32[1,192,256]{1,2,0:T(8,128)S(1)}, u32[]{:S(2)}) copy-start(f32[1,192,256]{1,2,0:T(8,128)S(1)} %get-tuple-element.58) | copy-start | bytes 589828
  27.5 6.1 %collective-permute-start.4 = (bf16[192,256]{0,1:T(8,128)(2,1)S(1)}, bf16[192,256]{0,1:T(8,128)(2,1)S(1)}, u32[]{:S(2)}, u32[]{:S(2)}) collective-permute-start(bf16[192,256]{0,1:T(8,128)(2,1)S(1)} %get-tuple-element.78), channel_id=1, source_target_pairs={{0,8},{8,16},{16,24},{24,32},{32,40},{40,48},{48,56},{56,64},{64,7... | collective-permute-start | bytes 294920 | tf_op jit(solution)/shard_map/ppermute | solution.py:12
  31.7 7.0 %collective-permute-start.5 = (bf16[192,256]{0,1:T(8,128)(2,1)S(1)}, bf16[192,256]{0,1:T(8,128)(2,1)S(1)}, u32[]{:S(2)}, u32[]{:S(2)}) collective-permute-start(bf16[192,256]{0,1:T(8,128)(2,1)S(1)} %get-tuple-element.79), channel_id=1, source_target_pairs={{0,1},{1,2},{2,3},{3,4},{4,5},{5,6},{6,7},{8,9},{9,10},{10,11},{11... | collective-permute-start | bytes 294920 | tf_op jit(solution)/shard_map/ppermute | solution.py:12
  33.7 6.1 %copy-start.1 = (bf16[1,1,768,768]{3,2,1,0:T(8,128)(2,1)S(1)}, bf16[1,1,768,768]{3,2,1,0:T(8,128)(2,1)}, u32[]{:S(2)}) copy-start(bf16[1,1,768,768]{3,2,1,0:T(8,128)(2,1)} %param.5) | copy-start | bytes 3538948
  41.5 12.1 %copy-start.3 = (f32[1,192,256]{1,2,0:T(8,128)S(1)}, f32[1,192,256]{1,2,0:T(8,128)}, u32[]{:S(2)}) copy-start(f32[1,192,256]{1,2,0:T(8,128)} %copy-done.2) | copy-start | bytes 589828
  41.5 12.1 %copy-start.5 = (f32[1,192,256]{1,2,0:T(8,128)S(1)}, f32[1,192,256]{1,2,0:T(8,128)}, u32[]{:S(2)}) copy-start(f32[1,192,256]{1,2,0:T(8,128)} %copy-done.4) | copy-start | bytes 589828
  41.5 8.1 %collective-permute-start.6 = (f32[192,256]{0,1:T(8,128)S(1)}, f32[192,256]{0,1:T(8,128)S(1)}, u32[]{:S(2)}, u32[]{:S(2)}) collective-permute-start(f32[192,256]{0,1:T(8,128)S(1)} %get-tuple-element.66), channel_id=1, source_target_pairs={{8,0},{16,8},{24,16},{32,24},{40,32},{48,40},{56,48},{64,56},{72,6... | collective-permute-start | bytes 589832 | tf_op jit(solution)/shard_map/ppermute | solution.py:12
  43.6 9.1 %collective-permute-start.7 = (f32[192,256]{0,1:T(8,128)S(1)}, f32[192,256]{0,1:T(8,128)S(1)}, u32[]{:S(2)}, u32[]{:S(2)}) collective-permute-start(f32[192,256]{0,1:T(8,128)S(1)} %get-tuple-element.67), channel_id=1, source_target_pairs={{1,0},{2,1},{3,2},{4,3},{5,4},{6,5},{7,6},{9,8},{10,9},{11,10},{12... | collective-permute-start | bytes 589832 | tf_op jit(solution)/shard_map/ppermute | solution.py:12
  171.6 6.2 %collective-permute-start.8 = (bf16[192,256]{0,1:T(8,128)(2,1)S(1)}, bf16[192,256]{0,1:T(8,128)(2,1)S(1)}, u32[]{:S(2)}, u32[]{:S(2)}) collective-permute-start(bf16[192,256]{0,1:T(8,128)(2,1)S(1)} %get-tuple-element.76), channel_id=1, source_target_pairs={{0,8},{8,16},{16,24},{24,32},{32,40},{40,48},{48,56},{56,64},{64,7... | collective-permute-start | bytes 294920 | tf_op jit(solution)/shard_map/ppermute | solution.py:12
  175.9 7.0 %collective-permute-start.9 = (bf16[192,256]{0,1:T(8,128)(2,1)S(1)}, bf16[192,256]{0,1:T(8,128)(2,1)S(1)}, u32[]{:S(2)}, u32[]{:S(2)}) collective-permute-start(bf16[192,256]{0,1:T(8,128)(2,1)S(1)} %get-tuple-element.77), channel_id=1, source_target_pairs={{0,1},{1,2},{2,3},{3,4},{4,5},{5,6},{6,7},{8,9},{9,10},{10,11},{11... | collective-permute-start | bytes 294920 | tf_op jit(solution)/shard_map/ppermute | solution.py:12
  187.4 8.0 %collective-permute-start.10 = (f32[192,256]{0,1:T(8,128)S(1)}, f32[192,256]{0,1:T(8,128)S(1)}, u32[]{:S(2)}, u32[]{:S(2)}) collective-permute-start(f32[192,256]{0,1:T(8,128)S(1)} %get-tuple-element.64), channel_id=1, source_target_pairs={{8,0},{16,8},{24,16},{32,24},{40,32},{48,40},{56,48},{64,56},{72,6... | collective-permute-start | bytes 589832 | tf_op jit(solution)/shard_map/ppermute | solution.py:12
  189.4 9.1 %collective-permute-start.11 = (f32[192,256]{0,1:T(8,128)S(1)}, f32[192,256]{0,1:T(8,128)S(1)}, u32[]{:S(2)}, u32[]{:S(2)}) collective-permute-start(f32[192,256]{0,1:T(8,128)S(1)} %get-tuple-element.65), channel_id=1, source_target_pairs={{1,0},{2,1},{3,2},{4,3},{5,4},{6,5},{7,6},{9,8},{10,9},{11,10},{12... | collective-permute-start | bytes 589832 | tf_op jit(solution)/shard_map/ppermute | solution.py:12
  199.4 0.7 copy-start.6
  199.4 0.8 copy-start.8
  200.2 6.7 %collective-permute-start.12 = (bf16[192,256]{0,1:T(8,128)(2,1)S(1)}, bf16[192,256]{0,1:T(8,128)(2,1)S(1)}, u32[]{:S(2)}, u32[]{:S(2)}) collective-permute-start(bf16[192,256]{0,1:T(8,128)(2,1)S(1)} %get-tuple-element.74), channel_id=1, source_target_pairs={{0,8},{8,16},{16,24},{24,32},{32,40},{40,48},{48,56},{56,64},{64,7... | collective-permute-start | bytes 294920 | tf_op jit(solution)/shard_map/ppermute | solution.py:12
  205.0 6.9 %collective-permute-start.13 = (bf16[192,256]{0,1:T(8,128)(2,1)S(1)}, bf16[192,256]{0,1:T(8,128)(2,1)S(1)}, u32[]{:S(2)}, u32[]{:S(2)}) collective-permute-start(bf16[192,256]{0,1:T(8,128)(2,1)S(1)} %get-tuple-element.75), channel_id=1, source_target_pairs={{0,1},{1,2},{2,3},{3,4},{4,5},{5,6},{6,7},{8,9},{9,10},{10,11},{11... | collective-permute-start | bytes 294920 | tf_op jit(solution)/shard_map/ppermute | solution.py:12
  216.5 11.6 %copy-start.7 = (f32[1,192,256]{1,2,0:T(8,128)S(1)}, f32[1,192,256]{1,2,0:T(8,128)}, u32[]{:S(2)}) copy-start(f32[1,192,256]{1,2,0:T(8,128)} %copy-done.6) | copy-start | bytes 589828
  216.5 11.6 %copy-start.9 = (f32[1,192,256]{1,2,0:T(8,128)S(1)}, f32[1,192,256]{1,2,0:T(8,128)}, u32[]{:S(2)}) copy-start(f32[1,192,256]{1,2,0:T(8,128)} %copy-done.8) | copy-start | bytes 589828
  216.5 8.1 %collective-permute-start.14 = (f32[192,256]{0,1:T(8,128)S(1)}, f32[192,256]{0,1:T(8,128)S(1)}, u32[]{:S(2)}, u32[]{:S(2)}) collective-permute-start(f32[192,256]{0,1:T(8,128)S(1)} %get-tuple-element.62), channel_id=1, source_target_pairs={{8,0},{16,8},{24,16},{32,24},{40,32},{48,40},{56,48},{64,56},{72,6... | collective-permute-start | bytes 589832 | tf_op jit(solution)/shard_map/ppermute | solution.py:12
  218.5 8.6 %collective-permute-start.15 = (f32[192,256]{0,1:T(8,128)S(1)}, f32[192,256]{0,1:T(8,128)S(1)}, u32[]{:S(2)}, u32[]{:S(2)}) collective-permute-start(f32[192,256]{0,1:T(8,128)S(1)} %get-tuple-element.63), channel_id=1, source_target_pairs={{1,0},{2,1},{3,2},{4,3},{5,4},{6,5},{7,6},{9,8},{10,9},{11,10},{12... | collective-permute-start | bytes 589832 | tf_op jit(solution)/shard_map/ppermute | solution.py:12
  228.0 0.7 copy-start.10
  228.0 0.8 copy-start.11
  339.0 4.1 collective-permute-start.16
  341.2 7.9 %collective-permute-start.17 = (bf16[192,256]{0,1:T(8,128)(2,1)S(1)}, bf16[192,256]{0,1:T(8,128)(2,1)S(1)}, u32[]{:S(2)}, u32[]{:S(2)}) collective-permute-start(bf16[192,256]{0,1:T(8,128)(2,1)S(1)} %get-tuple-element.73), channel_id=1, source_target_pairs={{0,1},{1,2},{2,3},{3,4},{4,5},{5,6},{6,7},{8,9},{9,10},{10,11},{11... | collective-permute-start | bytes 294920 | tf_op jit(solution)/shard_map/ppermute | solution.py:12
  351.8 7.7 %collective-permute-start.18 = (f32[192,256]{0,1:T(8,128)S(1)}, f32[192,256]{0,1:T(8,128)S(1)}, u32[]{:S(2)}, u32[]{:S(2)}) collective-permute-start(f32[192,256]{0,1:T(8,128)S(1)} %slice.207), channel_id=1, source_target_pairs={{8,0},{16,8},{24,16},{32,24},{40,32},{48,40},{56,48},{64,56},{72,6... | collective-permute-start | bytes 589832 | tf_op jit(solution)/shard_map/ppermute | solution.py:12
  360.2 7.2 %collective-permute-start.19 = (f32[192,256]{0,1:T(8,128)S(1)}, f32[192,256]{0,1:T(8,128)S(1)}, u32[]{:S(2)}, u32[]{:S(2)}) collective-permute-start(f32[192,256]{0,1:T(8,128)S(1)} %get-tuple-element.57), channel_id=1, source_target_pairs={{1,0},{2,1},{3,2},{4,3},{5,4},{6,5},{7,6},{9,8},{10,9},{11,10},{12... | collective-permute-start | bytes 589832 | tf_op jit(solution)/shard_map/ppermute | solution.py:12
  368.3 6.8 %collective-permute-start.20 = (bf16[192,256]{0,1:T(8,128)(2,1)S(1)}, bf16[192,256]{0,1:T(8,128)(2,1)S(1)}, u32[]{:S(2)}, u32[]{:S(2)}) collective-permute-start(bf16[192,256]{0,1:T(8,128)(2,1)S(1)} %get-tuple-element.70), channel_id=1, source_target_pairs={{0,8},{8,16},{16,24},{24,32},{32,40},{40,48},{48,56},{56,64},{64,7... | collective-permute-start | bytes 294920 | tf_op jit(solution)/shard_map/ppermute | solution.py:12
  373.2 6.9 %collective-permute-start.21 = (bf16[192,256]{0,1:T(8,128)(2,1)S(1)}, bf16[192,256]{0,1:T(8,128)(2,1)S(1)}, u32[]{:S(2)}, u32[]{:S(2)}) collective-permute-start(bf16[192,256]{0,1:T(8,128)(2,1)S(1)} %get-tuple-element.71), channel_id=1, source_target_pairs={{0,1},{1,2},{2,3},{3,4},{4,5},{5,6},{6,7},{8,9},{9,10},{10,11},{11... | collective-permute-start | bytes 294920 | tf_op jit(solution)/shard_map/ppermute | solution.py:12
  384.7 11.4 %copy-start.12 = (f32[2,192,256]{1,2,0:T(8,128)S(1)}, f32[2,192,256]{1,2,0:T(8,128)}, u32[]{:S(2)}) copy-start(f32[2,192,256]{1,2,0:T(8,128)} %get-tuple-element.21) | copy-start | bytes 1179652
  384.8 9.0 %collective-permute-start.22 = (f32[192,256]{0,1:T(8,128)S(1)}, f32[192,256]{0,1:T(8,128)S(1)}, u32[]{:S(2)}, u32[]{:S(2)}) collective-permute-start(f32[192,256]{0,1:T(8,128)S(1)} %get-tuple-element.55), channel_id=1, source_target_pairs={{8,0},{16,8},{24,16},{32,24},{40,32},{48,40},{56,48},{64,56},{72,6... | collective-permute-start | bytes 589832 | tf_op jit(solution)/shard_map/ppermute | solution.py:12
  386.8 8.4 %collective-permute-start.23 = (f32[192,256]{0,1:T(8,128)S(1)}, f32[192,256]{0,1:T(8,128)S(1)}, u32[]{:S(2)}, u32[]{:S(2)}) collective-permute-start(f32[192,256]{0,1:T(8,128)S(1)} %get-tuple-element.56), channel_id=1, source_target_pairs={{1,0},{2,1},{3,2},{4,3},{5,4},{6,5},{7,6},{9,8},{10,9},{11,10},{12... | collective-permute-start | bytes 589832 | tf_op jit(solution)/shard_map/ppermute | solution.py:12
where the time goes:
time: 513 us; the launch traced here: 512 us
  blocking collectives  337 us (66%)
  waiting for transfers between devices  76.2 us (15%)
  starting transfers between devices  60.6 us (12%)
  other arithmetic  15.7 us (3%)
  local copies, waits for them, and re-layouts  13.2 us (3%)
  matrix products  8.06 us (2%)
    psum x3, blocking collectives, column_sums(): return lax.psum((gamma_part, curve_part), ('wide', 'tile'))  337 us
    ppermute x24, waiting for transfers between devices, shifted(): return lax.ppermute(block, axis, route)  76.2 us
    ppermute x24, starting transfers between devices, shifted(): return lax.ppermute(block, axis, route)  60.6 us
  transfers between devices with their start and end apart: 24, of which 18 were waited for; matrix products, arithmetic and copies ran while one was open for 0% of the time, Pallas kernels for 0%

commit v1 on v0

v1 whole, which is shorter than its diff:
```python
import functools
import jax
import jax.numpy as jnp
from jax import lax
from jax.experimental import pallas as pl
from jax.experimental.pallas import tpu as pltpu
from jax.sharding import Mesh, PartitionSpec as P

ITERS = 3
CHUNK = 32
F32, BF16 = jnp.float32, jnp.bfloat16
VMEM = pl.BlockSpec(memory_space=pltpu.VMEM)
SMEM = pl.BlockSpec(memory_space=pltpu.SMEM)
WIDE = ("z", "x", "core")


def shifted(block, axis, distance):
    size = lax.axis_size(axis)
    route = [(i - distance, i) for i in range(size) if 0 <= i - distance < size]
    return lax.ppermute(block, axis, route)


def exchange(faces):
    below_tile = shifted(faces[1], "y", 1)
    above_tile = shifted(faces[3], "y", -1)
    below_wide = shifted(faces[0], WIDE, 1)
    above_wide = shifted(faces[2], WIDE, -1)
    return above_wide, above_tile, below_wide, below_tile


def pieces(rows):
    return [slice(start, start + CHUNK) for start in range(0, rows, CHUNK)]


def row_mask(start, count, columns):
    index = lax.broadcasted_iota(jnp.int32, (CHUNK, columns), 0) + start
    return index < count


def folded(block):
    return jnp.sum(block.reshape(block.shape[0] // 8, 8, block.shape[1]), axis=0)


def multiply(matrix_ref, lifted_ref, vector_at, faces, product_ref):
    rows, columns = faces[0].shape
    product_ref[...] = jnp.dot(matrix_ref[...], lifted_ref[...], preferred_element_type=F32)
    totals = [jnp.zeros((8, columns), F32), jnp.zeros((8, columns), F32)]
    for face in range(4):
        for piece in pieces(rows):
            whole = slice(face * rows + piece.start, face * rows + piece.stop)
            value = product_ref[whole, :]
            faces[face][piece, :] = value
            totals[face // 2] += folded(vector_at(face, piece) * value)
    return jnp.sum(totals[0] - totals[1], axis=0, keepdims=True)


def first_kernel(counts, matrix, gaps, below_wide, below_tile, res, gamma, f0, f1, f2, f3, lifted, product):
    rows, columns = below_wide.shape
    for face in range(4):
        for piece in pieces(rows):
            if face < 2:
                value = gaps[face, piece, :]
            else:
                value = (below_wide, below_tile)[face - 2][piece, :]
            value = jnp.where(row_mask(piece.start, counts[face], columns), value, 0.0)
            res[face, piece, :] = value
            signed = value if face < 2 else -value
            lifted[face * rows + piece.start : face * rows + piece.stop, :] = signed.astype(BF16)
    gamma[...] = multiply(matrix, lifted, lambda f, p: res[f, p, :], (f0, f1, f2, f3), product)


def assembled(face, piece, own, across, count):
    value = own[face][piece, :] - across[face][piece, :]
    if face >= 2:
        value = -value
    return jnp.where(row_mask(piece.start, count, value.shape[1]), value, 0.0)


def flex_kernel(counts, matrix, y0, y1, y2, y3, a0, a1, b0, b1, gamma, pre, sums, f0, f1, f2, f3, lifted, product):
    rows, columns = y0.shape
    own, across = (y0, y1, y2, y3), (a0, a1, b0, b1)
    for face in range(4):
        for piece in pieces(rows):
            value = assembled(face, piece, own, across, counts[face])
            pre[face, piece, :] = value
            signed = value if face < 2 else -value
            lifted[face * rows + piece.start : face * rows + piece.stop, :] = signed.astype(BF16)
    sums[0:1, :] = gamma[...]
    sums[1:2, :] = multiply(matrix, lifted, lambda f, p: pre[f, p, :], (f0, f1, f2, f3), product)


def step_sizes(first, sums, scal):
    gamma, curvature = sums[0:1, :], sums[1:2, :]
    if first:
        return gamma, gamma / curvature, None
    scaling = gamma / scal[0:1, :]
    return gamma, gamma / (curvature - scaling * gamma / scal[1:2, :]), scaling


def update_kernel(first, *refs):
    (counts, matrix, sums, y0, y1, y2, y3, a0, a1, b0, b1, pre, res), refs = refs[:13], refs[13:]
    if not first:
        (scal, direction, along, mult), refs = refs[:4], refs[4:]
    res_out, direction_out, along_out, mult_out, scal_out, gamma_out, f0, f1, f2, f3, lifted, product = refs
    rows, columns = y0.shape
    gamma, step, scaling = step_sizes(first, sums, None if first else scal)
    scal_out[0:1, :] = gamma
    scal_out[1:2, :] = step
    own, across = (y0, y1, y2, y3), (a0, a1, b0, b1)
    for face in range(4):
        for piece in pieces(rows):
            mapped = assembled(face, piece, own, across, counts[face])
            if not first:
                mapped = mapped + scaling * along[face, piece, :]
            along_out[face, piece, :] = mapped
            value = res[face, piece, :] - step * mapped
            res_out[face, piece, :] = value
            signed = value if face < 2 else -value
            lifted[face * rows + piece.start : face * rows + piece.stop, :] = signed.astype(BF16)
            if face < 2:
                way = pre[face, piece, :]
                if not first:
                    way = way + scaling * direction[face, piece, :]
                direction_out[face, piece, :] = way
                moved = step * way
                mult_out[face, piece, :] = moved if first else mult[face, piece, :] + moved
    gamma_out[...] = multiply(matrix, lifted, lambda f, p: res_out[f, p, :], (f0, f1, f2, f3), product)


def last_kernel(counts, sums, y0, y1, a0, a1, pre, res, scal, direction, along, mult, mult_out, res_out):
    rows, columns = y0.shape
    gamma, step, scaling = step_sizes(False, sums, scal)
    for face in range(2):
        for piece in pieces(rows):
            mapped = assembled(face, piece, (y0, y1), (a0, a1), counts[face])
            mapped = mapped + scaling * along[face, piece, :]
            res_out[face, piece, :] = res[face, piece, :] - step * mapped
            way = pre[face, piece, :] + scaling * direction[face, piece, :]
            mult_out[face, piece, :] = mult[face, piece, :] + step * way


def call(kernel, outs, args, name, size=None):
    scratch = []
    flops = 0
    if size is not None:
        rows, columns = size
        scratch = [pltpu.VMEM((rows, columns), BF16), pltpu.VMEM((rows, columns), F32)]
        flops = 2 * rows * rows * columns
    moved = sum(a.size * a.dtype.itemsize for a in args) + 4 * sum(o.size for o in outs)
    return pl.pallas_call(
        kernel,
        out_shape=outs,
        in_specs=[SMEM] + [VMEM] * (len(args) - 1),
        out_specs=[VMEM] * len(outs),
        scratch_shapes=scratch,
        name=name,
        cost_estimate=pl.CostEstimate(flops=flops, bytes_accessed=moved, transcendentals=0),
        compiler_params=pltpu.CompilerParams(vmem_limit_bytes=24 * 1024 * 1024),
    )(*args)


def total(sums, stages):
    for axes in stages:
        sums = lax.optimization_barrier(lax.psum(sums, axes))
    return sums


STAGES = (
    ("y", "z", ("x", "core")),
    ("y", "z", "x", "core"),
    (("core", "y"), "x", "z"),
)


def per_device(interface_gaps, flexibility, dirichlet_schur, face_rows):
    rows, columns = interface_gaps.shape[3:]
    counts = face_rows[0, 0]
    flex, schur = flexibility[0, 0], dirichlet_schur[0, 0]
    gaps = interface_gaps[0, 0]
    size = (4 * rows, columns)
    four = jax.ShapeDtypeStruct((4, rows, columns), F32)
    two = jax.ShapeDtypeStruct((2, rows, columns), F32)
    face = jax.ShapeDtypeStruct((rows, columns), F32)
    line = jax.ShapeDtypeStruct((1, columns), F32)
    pair = jax.ShapeDtypeStruct((2, columns), F32)
    faces = [face] * 4

    below_tile = shifted(gaps[1], "y", 1)
    below_wide = shifted(gaps[0], WIDE, 1)
    res, gamma, *out = call(
        first_kernel, [four, line] + faces, [counts, schur, gaps, below_wide, below_tile], "first", size
    )
    state = []
    for iteration in range(ITERS):
        across = exchange(out)
        pre, sums, *out = call(
            flex_kernel, [four, pair] + faces, [counts, flex, *out, *across, gamma], "flex", size
        )
        if iteration + 1 < ITERS:
            across = exchange(out)
            sums = total(sums, STAGES[iteration])
            res, direction, along, mult, scal, gamma, *out = call(
                functools.partial(update_kernel, iteration == 0),
                [four, two, four, two, pair, line] + faces,
                [counts, schur, sums, *out, *across, pre, res, *state],
                "update",
                size,
            )
            state = [scal, direction, along, mult]
        else:
            above_tile = shifted(out[3], "y", -1)
            above_wide = shifted(out[2], WIDE, -1)
            sums = total(sums, STAGES[iteration])
            mult, res = call(
                last_kernel, [two, two], [counts, sums, out[0], out[1], above_wide, above_tile, pre, res, *state], "last"
            )
    return mult[None, None], res[None, None]


def solution(mesh):
    wide, tile = mesh.devices.shape
    split = Mesh(mesh.devices.reshape(wide // 8, 4, 2, tile), ("z", "x", "core", "y"))
    placed = (
        P(WIDE, "y", None, None, None),
        P(WIDE, "y", None, None),
        P(WIDE, "y", None, None),
        P(WIDE, "y", None),
    )
    return jax.shard_map(
        per_device,
        mesh=split,
        in_specs=placed,
        out_specs=(P(WIDE, "y", None, None, None), P(WIDE, "y", None, None, None)),
        check_vma=False,
    )
```

time: 513 us -> 315 us (0.61)
  the two profiles are of different devices: /device:TPU:33 before, /device:TPU:2 now
where the time goes in v1:
time: 315 us; the launch traced here: 314 us
  blocking collectives  189 us (60%)
  starting transfers between devices  59.5 us (19%)
  local copies, waits for them, and re-layouts  28.1 us (9%)
  waiting for transfers between devices  25.2 us (8%)
  Pallas kernels  10.9 us (3%)
    psum x10, blocking collectives, total(): sums = lax.optimization_barrier(lax.psum(sums, axes))  189 us
    ppermute x24, starting transfers between devices, shifted(): return lax.ppermute(block, axis, route)  59.5 us
    unnamed x76, local copies, waits for them, and re-layouts  27.1 us
    ppermute x24, waiting for transfers between devices, shifted(): return lax.ppermute(block, axis, route)  25.2 us
    pallas_call x7, Pallas kernels, call(): pl.pallas_call(kernel, out_shape=outs, in_specs=[SMEM] + [VMEM] * (len(ar...  10.9 us
  transfers between devices with their start and end apart: 24, of which 8 were waited for; matrix products, arithmetic and copies ran while one was open for 0% of the time, Pallas kernels for 0%

profile of v1, /device:TPU:2, one launch (start us, length us, event | category | flops | bytes accessed | tf_op | source)
XLA Modules:
  0.0 313.8 jit_solution(4154241296834516867)
XLA Ops:
  1.7 3.6 %collective-permute-start.1 = (f32[192,256]{1,0:T(8,128)S(1)}, f32[192,256]{1,0:T(8,128)S(1)}, u32[]{:S(2)}, u32[]{:S(2)}) collective-permute-start(f32[192,256]{1,0:T(8,128)S(1)} %get-tuple-element.94), channel_id=1, source_target_pairs={{0,1},{1,2},{2,3},{3,4},{4,5},{5,6},{6,7},{8,9},{9,10},{10,11},{11... | collective-permute-start | bytes 589832 | tf_op jit(solution)/shard_map/ppermute | solution.py:20
  5.3 1.9 collective-permute-start
  7.3 2.2 collective-permute-done.1.below_tile
  9.5 2.9 collective-permute-done.below_wide
  12.3 1.3 copy-done.1
  16.3 1.9 collective-permute-start.4
  18.2 3.5 %collective-permute-start.5 = (f32[192,256]{1,0:T(8,128)S(1)}, f32[192,256]{1,0:T(8,128)S(1)}, u32[]{:S(2)}, u32[]{:S(2)}) collective-permute-start(f32[192,256]{1,0:T(8,128)S(1)} %get-tuple-element.49.y1), channel_id=1, source_target_pairs={{0,1},{1,2},{2,3},{3,4},{4,5},{5,6},{6,7},{8,9},{9,10},{10,11},{11... | collective-permute-start | bytes 589832 | tf_op jit(solution)/shard_map/ppermute | solution.py:20
  21.7 3.4 %collective-permute-start.2 = (f32[192,256]{1,0:T(8,128)S(1)}, f32[192,256]{1,0:T(8,128)S(1)}, u32[]{:S(2)}, u32[]{:S(2)}) collective-permute-start(f32[192,256]{1,0:T(8,128)S(1)} %get-tuple-element.50.y2), channel_id=1, source_target_pairs={{8,0},{16,8},{24,16},{32,24},{40,32},{48,40},{56,48},{64,56},{72,6... | collective-permute-start | bytes 589832 | tf_op jit(solution)/shard_map/ppermute | solution.py:20
  25.1 1.3 collective-permute-start.3
  26.4 1.8 collective-permute-done.2.a0
  28.3 5.4 %collective-permute-done.3.a1 = f32[192,256]{1,0:T(8,128)S(1)} collective-permute-done((f32[192,256]{1,0:T(8,128)S(1)}, f32[192,256]{1,0:T(8,128)S(1)}, u32[]{:S(2)}, u32[]{:S(2)}) %collective-permute-start.3) | collective-permute-done | bytes 196640 | tf_op jit(solution)/shard_map/ppermute | solution.py:20
  33.7 1.8 flex.3
  36.3 1.9 collective-permute-start.8
  38.3 5.2 %collective-permute-start.9 = (f32[192,256]{1,0:T(8,128)S(1)}, f32[192,256]{1,0:T(8,128)}, u32[]{:S(2)}, u32[]{:S(2)}) collective-permute-start(f32[192,256]{1,0:T(8,128)S(1)} %get-tuple-element.55.refs_4_), channel_id=1, source_target_pairs={{0,1},{1,2},{2,3},{3,4},{4,5},{5,6},{6,7},{8,9},{9,10},{10,11},{11... | collective-permute-start | bytes 589832 | tf_op jit(solution)/shard_map/ppermute | solution.py:20
  43.5 3.4 %collective-permute-start.6 = (f32[192,256]{1,0:T(8,128)}, f32[192,256]{1,0:T(8,128)}, u32[]{:S(2)}, u32[]{:S(2)}) collective-permute-start(f32[192,256]{1,0:T(8,128)} %get-tuple-element.56.refs_5_), channel_id=1, source_target_pairs={{8,0},{16,8},{24,16},{32,24},{40,32},{48,40},{56,48},{64,56},{72,6... | collective-permute-start | bytes 589832 | tf_op jit(solution)/shard_map/ppermute | solution.py:20
  46.8 1.3 collective-permute-start.7
  48.1 16.8 %psum.70 = f32[2,256]{1,0:T(2,128)S(1)} all-reduce(f32[2,256]{1,0:T(2,128)S(1)} %get-tuple-element.53), channel_id=1, replica_groups=mesh['z'=12,'x'=4,'core'=2,'y'=8] {'y'}, use_global_device_ids=true, to_apply=%region_0.0 | all-reduce | flops 512 | bytes 4096 | tf_op jit(solution)/shard_map/psum | solution.py:164
  64.9 33.3 %psum.71 = f32[2,256]{1,0:T(2,128)S(1)} all-reduce(f32[2,256]{1,0:T(2,128)S(1)} %psum.70), channel_id=1, replica_groups=mesh['z'=12,'x'=4,'core'=2,'y'=8] {'z'}, use_global_device_ids=true, to_apply=%region_1.0 | all-reduce | flops 512 | bytes 4096 | tf_op jit(solution)/shard_map/psum | solution.py:164
  98.2 14.5 %psum.72.refs_2_ = f32[2,256]{1,0:T(2,128)S(1)} all-reduce(f32[2,256]{1,0:T(2,128)S(1)} %psum.71), channel_id=1, replica_groups=mesh['z'=12,'x'=4,'core'=2,'y'=8] {'x','core'}, use_global_device_ids=true, to_apply=%region_2.0 | all-reduce | flops 512 | bytes 4096 | tf_op jit(solution)/shard_map/psum | solution.py:164
  113.9 2.0 update.2
  116.8 1.9 collective-permute-start.12
  118.7 2.2 collective-permute-start.13
  120.9 4.6 %collective-permute-start.10 = (f32[192,256]{1,0:T(8,128)S(1)}, f32[192,256]{1,0:T(8,128)S(1)}, u32[]{:S(2)}, u32[]{:S(2)}) collective-permute-start(f32[192,256]{1,0:T(8,128)S(1)} %get-tuple-element.62.y2), channel_id=1, source_target_pairs={{8,0},{16,8},{24,16},{32,24},{40,32},{48,40},{56,48},{64,56},{72,6... | collective-permute-start | bytes 589832 | tf_op jit(solution)/shard_map/ppermute | solution.py:20
  125.5 1.3 collective-permute-start.11
  126.8 1.8 collective-permute-done.10.a0
  128.6 4.4 %collective-permute-done.11.a1 = f32[192,256]{1,0:T(8,128)S(1)} collective-permute-done((f32[192,256]{1,0:T(8,128)S(1)}, f32[192,256]{1,0:T(8,128)S(1)}, u32[]{:S(2)}, u32[]{:S(2)}) %collective-permute-start.11) | collective-permute-done | bytes 196640 | tf_op jit(solution)/shard_map/ppermute | solution.py:20
  135.1 1.9 collective-permute-start.16
  137.7 3.6 %collective-permute-start.17 = (f32[192,256]{1,0:T(8,128)S(1)}, f32[192,256]{1,0:T(8,128)S(1)}, u32[]{:S(2)}, u32[]{:S(2)}) collective-permute-start(f32[192,256]{1,0:T(8,128)S(1)} %get-tuple-element.67.refs_4_), channel_id=1, source_target_pairs={{0,1},{1,2},{2,3},{3,4},{4,5},{5,6},{6,7},{8,9},{9,10},{10,11},{11... | collective-permute-start | bytes 589832 | tf_op jit(solution)/shard_map/ppermute | solution.py:20
  142.0 3.4 %collective-permute-start.14 = (f32[192,256]{1,0:T(8,128)S(1)}, f32[192,256]{1,0:T(8,128)}, u32[]{:S(2)}, u32[]{:S(2)}) collective-permute-start(f32[192,256]{1,0:T(8,128)S(1)} %get-tuple-element.68.refs_5_), channel_id=1, source_target_pairs={{8,0},{16,8},{24,16},{32,24},{40,32},{48,40},{56,48},{64,56},{72,6... | collective-permute-start | bytes 589832 | tf_op jit(solution)/shard_map/ppermute | solution.py:20
  146.0 1.3 collective-permute-start.15
  148.0 19.2 %psum.73 = f32[2,256]{1,0:T(2,128)S(1)} all-reduce(f32[2,256]{1,0:T(2,128)S(1)} %get-tuple-element.65), channel_id=1, replica_groups=mesh['z'=12,'x'=4,'core'=2,'y'=8] {'y'}, use_global_device_ids=true, to_apply=%region_3.0 | all-reduce | flops 512 | bytes 4096 | tf_op jit(solution)/shard_map/psum | solution.py:164
  167.2 22.6 %psum.74 = f32[2,256]{1,0:T(2,128)S(1)} all-reduce(f32[2,256]{1,0:T(2,128)S(1)} %psum.73), channel_id=1, replica_groups=mesh['z'=12,'x'=4,'core'=2,'y'=8] {'z'}, use_global_device_ids=true, to_apply=%region_4.0 | all-reduce | flops 512 | bytes 4096 | tf_op jit(solution)/shard_map/psum | solution.py:164
  189.8 14.2 %psum.75 = f32[2,256]{1,0:T(2,128)S(1)} all-reduce(f32[2,256]{1,0:T(2,128)S(1)} %psum.74), channel_id=1, replica_groups=mesh['z'=12,'x'=4,'core'=2,'y'=8] {'x'}, use_global_device_ids=true, to_apply=%region_5.0 | all-reduce | flops 512 | bytes 4096 | tf_op jit(solution)/shard_map/psum | solution.py:164
  204.0 2.5 psum.76.refs_2_
  218.8 1.8 update.3
  220.6 2.1 collective-permute-start.20
  222.7 2.2 collective-permute-start.21
  224.9 3.2 %collective-permute-start.18 = (f32[192,256]{1,0:T(8,128)S(1)}, f32[192,256]{1,0:T(8,128)S(1)}, u32[]{:S(2)}, u32[]{:S(2)}) collective-permute-start(f32[192,256]{1,0:T(8,128)S(1)} %get-tuple-element.78.y2), channel_id=1, source_target_pairs={{8,0},{16,8},{24,16},{32,24},{40,32},{48,40},{56,48},{64,56},{72,6... | collective-permute-start | bytes 589832 | tf_op jit(solution)/shard_map/ppermute | solution.py:20
  228.1 1.3 collective-permute-start.19
  229.4 1.8 collective-permute-done.18.a0
  231.3 4.7 %collective-permute-done.19.a1 = f32[192,256]{1,0:T(8,128)S(1)} collective-permute-done((f32[192,256]{1,0:T(8,128)S(1)}, f32[192,256]{1,0:T(8,128)S(1)}, u32[]{:S(2)}, u32[]{:S(2)}) %collective-permute-start.19) | collective-permute-done | bytes 196640 | tf_op jit(solution)/shard_map/ppermute | solution.py:20
  236.0 1.7 flex.5
  239.1 1.9 collective-permute-start.22
  241.0 1.3 collective-permute-start.23
  242.3 33.4 %psum.77 = f32[2,256]{1,0:T(2,128)S(1)} all-reduce(f32[2,256]{1,0:T(2,128)S(1)} %get-tuple-element.81), channel_id=1, replica_groups=mesh['z'=12,'x'=4,'core'=2,'y'=8] {'core','y'}, use_global_device_ids=true, to_apply=%region_7.0 | all-reduce | flops 512 | bytes 4096 | tf_op jit(solution)/shard_map/psum | solution.py:164
  275.7 7.7 %psum.78 = f32[2,256]{1,0:T(2,128)S(1)} all-reduce(f32[2,256]{1,0:T(2,128)S(1)} %psum.77), channel_id=1, replica_groups=mesh['z'=12,'x'=4,'core'=2,'y'=8] {'x'}, use_global_device_ids=true, to_apply=%region_8.0 | all-reduce | flops 512 | bytes 4096 | tf_op jit(solution)/shard_map/psum | solution.py:164
  283.4 24.8 %psum.79.sums = f32[2,256]{1,0:T(2,128)S(1)} all-reduce(f32[2,256]{1,0:T(2,128)S(1)} %psum.78), channel_id=1, replica_groups=mesh['z'=12,'x'=4,'core'=2,'y'=8] {'z'}, use_global_device_ids=true, to_apply=%region_9.0 | all-reduce | flops 512 | bytes 4096 | tf_op jit(solution)/shard_map/psum | solution.py:164
  312.2 1.6 last.1
  (94 shorter events, 29.0 us)
Async XLA Ops:
  1.7 32.0 %copy-start = (bf16[1,1,768,768]{3,2,1,0:T(8,128)(2,1)S(1)}, bf16[1,1,768,768]{3,2,1,0:T(8,128)(2,1)}, u32[]{:S(2)}) copy-start(bf16[1,1,768,768]{3,2,1,0:T(8,128)(2,1)} %param.5) | copy-start | bytes 3538948
  1.7 7.8 %collective-permute-start.1 = (f32[192,256]{1,0:T(8,128)S(1)}, f32[192,256]{1,0:T(8,128)S(1)}, u32[]{:S(2)}, u32[]{:S(2)}) collective-permute-start(f32[192,256]{1,0:T(8,128)S(1)} %get-tuple-element.94), channel_id=1, source_target_pairs={{0,1},{1,2},{2,3},{3,4},{4,5},{5,6},{6,7},{8,9},{9,10},{10,11},{11... | collective-permute-start | bytes 589832 | tf_op jit(solution)/shard_map/ppermute | solution.py:20
  5.3 7.0 %collective-permute-start = (f32[192,256]{1,0:T(8,128)S(1)}, f32[192,256]{1,0:T(8,128)S(1)}, u32[]{:S(2)}, u32[]{:S(2)}) collective-permute-start(f32[192,256]{1,0:T(8,128)S(1)} %get-tuple-element.95), channel_id=1, source_target_pairs={{0,8},{8,16},{16,24},{24,32},{32,40},{40,48},{48,56},{56,64},{64,7... | collective-permute-start | bytes 589832 | tf_op jit(solution)/shard_map/ppermute | solution.py:20
  12.3 1.3 copy-start.1
  13.6 1.0 copy-start.3
  16.3 10.1 %collective-permute-start.4 = (f32[192,256]{1,0:T(8,128)S(1)}, f32[192,256]{1,0:T(8,128)S(1)}, u32[]{:S(2)}, u32[]{:S(2)}) collective-permute-start(f32[192,256]{1,0:T(8,128)S(1)} %get-tuple-element.48.y0), channel_id=1, source_target_pairs={{0,8},{8,16},{16,24},{24,32},{32,40},{40,48},{48,56},{56,64},{64,7... | collective-permute-start | bytes 589832 | tf_op jit(solution)/shard_map/ppermute | solution.py:20
  18.2 8.2 %collective-permute-start.5 = (f32[192,256]{1,0:T(8,128)S(1)}, f32[192,256]{1,0:T(8,128)S(1)}, u32[]{:S(2)}, u32[]{:S(2)}) collective-permute-start(f32[192,256]{1,0:T(8,128)S(1)} %get-tuple-element.49.y1), channel_id=1, source_target_pairs={{0,1},{1,2},{2,3},{3,4},{4,5},{5,6},{6,7},{8,9},{9,10},{10,11},{11... | collective-permute-start | bytes 589832 | tf_op jit(solution)/shard_map/ppermute | solution.py:20
  21.7 6.5 %collective-permute-start.2 = (f32[192,256]{1,0:T(8,128)S(1)}, f32[192,256]{1,0:T(8,128)S(1)}, u32[]{:S(2)}, u32[]{:S(2)}) collective-permute-start(f32[192,256]{1,0:T(8,128)S(1)} %get-tuple-element.50.y2), channel_id=1, source_target_pairs={{8,0},{16,8},{24,16},{32,24},{40,32},{48,40},{56,48},{64,56},{72,6... | collective-permute-start | bytes 589832 | tf_op jit(solution)/shard_map/ppermute | solution.py:20
  25.1 8.6 %collective-permute-start.3 = (f32[192,256]{1,0:T(8,128)S(1)}, f32[192,256]{1,0:T(8,128)S(1)}, u32[]{:S(2)}, u32[]{:S(2)}) collective-permute-start(f32[192,256]{1,0:T(8,128)S(1)} %get-tuple-element.51.y3), channel_id=1, source_target_pairs={{1,0},{2,1},{3,2},{4,3},{5,4},{6,5},{7,6},{9,8},{10,9},{11,10},{12... | collective-permute-start | bytes 589832 | tf_op jit(solution)/shard_map/ppermute | solution.py:20
  33.7 79.1 %copy-start.2 = (bf16[1,1,768,768]{3,2,1,0:T(8,128)(2,1)S(1)}, bf16[1,1,768,768]{3,2,1,0:T(8,128)(2,1)}, u32[]{:S(2)}) copy-start(bf16[1,1,768,768]{3,2,1,0:T(8,128)(2,1)} %param.6) | copy-start | bytes 3538948
  33.7 79.1 %copy-start.37 = (s32[1,1,4]{2,1,0:T(1,128)S(1)}, s32[1,1,4]{2,1,0:T(1,128)}, u32[]{:S(2)}) copy-start(s32[1,1,4]{2,1,0:T(1,128)} %param.7) | copy-start | bytes 52
  36.3 76.4 %collective-permute-start.8 = (f32[192,256]{1,0:T(8,128)S(1)}, f32[192,256]{1,0:T(8,128)}, u32[]{:S(2)}, u32[]{:S(2)}) collective-permute-start(f32[192,256]{1,0:T(8,128)S(1)} %get-tuple-element.54.refs_3_), channel_id=1, source_target_pairs={{0,8},{8,16},{16,24},{24,32},{32,40},{40,48},{48,56},{56,64},{64,7... | collective-permute-start | bytes 589832 | tf_op jit(solution)/shard_map/ppermute | solution.py:20
  38.3 74.5 %collective-permute-start.9 = (f32[192,256]{1,0:T(8,128)S(1)}, f32[192,256]{1,0:T(8,128)}, u32[]{:S(2)}, u32[]{:S(2)}) collective-permute-start(f32[192,256]{1,0:T(8,128)S(1)} %get-tuple-element.55.refs_4_), channel_id=1, source_target_pairs={{0,1},{1,2},{2,3},{3,4},{4,5},{5,6},{6,7},{8,9},{9,10},{10,11},{11... | collective-permute-start | bytes 589832 | tf_op jit(solution)/shard_map/ppermute | solution.py:20
  43.5 69.2 %collective-permute-start.6 = (f32[192,256]{1,0:T(8,128)}, f32[192,256]{1,0:T(8,128)}, u32[]{:S(2)}, u32[]{:S(2)}) collective-permute-start(f32[192,256]{1,0:T(8,128)} %get-tuple-element.56.refs_5_), channel_id=1, source_target_pairs={{8,0},{16,8},{24,16},{32,24},{40,32},{48,40},{56,48},{64,56},{72,6... | collective-permute-start | bytes 589832 | tf_op jit(solution)/shard_map/ppermute | solution.py:20
  46.8 65.9 %collective-permute-start.7 = (f32[192,256]{1,0:T(8,128)}, f32[192,256]{1,0:T(8,128)}, u32[]{:S(2)}, u32[]{:S(2)}) collective-permute-start(f32[192,256]{1,0:T(8,128)} %get-tuple-element.57.refs_6_), channel_id=1, source_target_pairs={{1,0},{2,1},{3,2},{4,3},{5,4},{6,5},{7,6},{9,8},{10,9},{11,10},{12... | collective-permute-start | bytes 589832 | tf_op jit(solution)/shard_map/ppermute | solution.py:20
  112.8 1.1 copy-start.13
  116.8 17.4 %copy-start.8 = (f32[4,192,256]{2,1,0:T(8,128)}, f32[4,192,256]{2,1,0:T(8,128)S(1)}, u32[]{:S(2)}) copy-start(f32[4,192,256]{2,1,0:T(8,128)S(1)} %get-tuple-element.74.refs_15_) | copy-start | bytes 2359300
  116.8 17.4 %copy-start.16 = (f32[2,192,256]{2,1,0:T(8,128)}, f32[2,192,256]{2,1,0:T(8,128)S(1)}, u32[]{:S(2)}) copy-start(f32[2,192,256]{2,1,0:T(8,128)S(1)} %get-tuple-element.73.refs_14_) | copy-start | bytes 1179652
  116.8 17.4 %copy-start.18 = (f32[2,192,256]{2,1,0:T(8,128)}, f32[2,192,256]{2,1,0:T(8,128)S(1)}, u32[]{:S(2)}) copy-start(f32[2,192,256]{2,1,0:T(8,128)S(1)} %get-tuple-element.75.refs_16_) | copy-start | bytes 1179652
  116.8 10.0 %collective-permute-start.12 = (f32[192,256]{1,0:T(8,128)S(1)}, f32[192,256]{1,0:T(8,128)S(1)}, u32[]{:S(2)}, u32[]{:S(2)}) collective-permute-start(f32[192,256]{1,0:T(8,128)S(1)} %get-tuple-element.60.y0), channel_id=1, source_target_pairs={{0,8},{8,16},{16,24},{24,32},{32,40},{40,48},{48,56},{56,64},{64,7... | collective-permute-start | bytes 589832 | tf_op jit(solution)/shard_map/ppermute | solution.py:20
  118.7 8.1 %collective-permute-start.13 = (f32[192,256]{1,0:T(8,128)S(1)}, f32[192,256]{1,0:T(8,128)S(1)}, u32[]{:S(2)}, u32[]{:S(2)}) collective-permute-start(f32[192,256]{1,0:T(8,128)S(1)} %get-tuple-element.61.y1), channel_id=1, source_target_pairs={{0,1},{1,2},{2,3},{3,4},{4,5},{5,6},{6,7},{8,9},{9,10},{10,11},{11... | collective-permute-start | bytes 589832 | tf_op jit(solution)/shard_map/ppermute | solution.py:20
  120.9 7.7 %collective-permute-start.10 = (f32[192,256]{1,0:T(8,128)S(1)}, f32[192,256]{1,0:T(8,128)S(1)}, u32[]{:S(2)}, u32[]{:S(2)}) collective-permute-start(f32[192,256]{1,0:T(8,128)S(1)} %get-tuple-element.62.y2), channel_id=1, source_target_pairs={{8,0},{16,8},{24,16},{32,24},{40,32},{48,40},{56,48},{64,56},{72,6... | collective-permute-start | bytes 589832 | tf_op jit(solution)/shard_map/ppermute | solution.py:20
  125.5 7.6 %collective-permute-start.11 = (f32[192,256]{1,0:T(8,128)S(1)}, f32[192,256]{1,0:T(8,128)S(1)}, u32[]{:S(2)}, u32[]{:S(2)}) collective-permute-start(f32[192,256]{1,0:T(8,128)S(1)} %get-tuple-element.63.y3), channel_id=1, source_target_pairs={{1,0},{2,1},{3,2},{4,3},{5,4},{6,5},{7,6},{9,8},{10,9},{11,10},{12... | collective-permute-start | bytes 589832 | tf_op jit(solution)/shard_map/ppermute | solution.py:20
  135.1 71.4 %collective-permute-start.16 = (f32[192,256]{1,0:T(8,128)S(1)}, f32[192,256]{1,0:T(8,128)S(1)}, u32[]{:S(2)}, u32[]{:S(2)}) collective-permute-start(f32[192,256]{1,0:T(8,128)S(1)} %get-tuple-element.66.refs_3_), channel_id=1, source_target_pairs={{0,8},{8,16},{16,24},{24,32},{32,40},{40,48},{48,56},{56,64},{64,7... | collective-permute-start | bytes 589832 | tf_op jit(solution)/shard_map/ppermute | solution.py:20
  137.7 69.5 %collective-permute-start.17 = (f32[192,256]{1,0:T(8,128)S(1)}, f32[192,256]{1,0:T(8,128)S(1)}, u32[]{:S(2)}, u32[]{:S(2)}) collective-permute-start(f32[192,256]{1,0:T(8,128)S(1)} %get-tuple-element.67.refs_4_), channel_id=1, source_target_pairs={{0,1},{1,2},{2,3},{3,4},{4,5},{5,6},{6,7},{8,9},{9,10},{10,11},{11... | collective-permute-start | bytes 589832 | tf_op jit(solution)/shard_map/ppermute | solution.py:20
  142.0 65.9 %collective-permute-start.14 = (f32[192,256]{1,0:T(8,128)S(1)}, f32[192,256]{1,0:T(8,128)}, u32[]{:S(2)}, u32[]{:S(2)}) collective-permute-start(f32[192,256]{1,0:T(8,128)S(1)} %get-tuple-element.68.refs_5_), channel_id=1, source_target_pairs={{8,0},{16,8},{24,16},{32,24},{40,32},{48,40},{56,48},{64,56},{72,6... | collective-permute-start | bytes 589832 | tf_op jit(solution)/shard_map/ppermute | solution.py:20
  146.0 61.8 %collective-permute-start.15 = (f32[192,256]{1,0:T(8,128)S(1)}, f32[192,256]{1,0:T(8,128)}, u32[]{:S(2)}, u32[]{:S(2)}) collective-permute-start(f32[192,256]{1,0:T(8,128)S(1)} %get-tuple-element.69.refs_6_), channel_id=1, source_target_pairs={{1,0},{2,1},{3,2},{4,3},{5,4},{6,5},{7,6},{9,8},{10,9},{11,10},{12... | collective-permute-start | bytes 589832 | tf_op jit(solution)/shard_map/ppermute | solution.py:20
  207.8 1.1 copy-start.7
  209.0 1.1 copy-start.9
  210.1 1.1 copy-start.11
  211.2 1.0 copy-start.17
  212.2 1.0 copy-start.19
  213.2 0.9 copy-start.25
  214.1 0.9 copy-start.27
  215.1 0.9 copy-start.29
  216.0 0.9 copy-start.31
  216.9 0.9 copy-start.33
  217.9 0.9 copy-start.35
  220.6 17.1 %copy-start.4 = (f32[4,192,256]{2,1,0:T(8,128)}, f32[4,192,256]{2,1,0:T(8,128)S(1)}, u32[]{:S(2)}) copy-start(f32[4,192,256]{2,1,0:T(8,128)S(1)} %get-tuple-element.90.along) | copy-start | bytes 2359300
  220.6 17.1 %copy-start.14 = (f32[2,192,256]{2,1,0:T(8,128)}, f32[2,192,256]{2,1,0:T(8,128)S(1)}, u32[]{:S(2)}) copy-start(f32[2,192,256]{2,1,0:T(8,128)S(1)} %get-tuple-element.91.mult) | copy-start | bytes 1179652
  220.6 8.8 %collective-permute-start.20 = (f32[192,256]{1,0:T(8,128)S(1)}, f32[192,256]{1,0:T(8,128)S(1)}, u32[]{:S(2)}, u32[]{:S(2)}) collective-permute-start(f32[192,256]{1,0:T(8,128)S(1)} %get-tuple-element.76.y0), channel_id=1, source_target_pairs={{0,8},{8,16},{16,24},{24,32},{32,40},{40,48},{48,56},{56,64},{64,7... | collective-permute-start | bytes 589832 | tf_op jit(solution)/shard_map/ppermute | solution.py:20
  222.7 6.7 %collective-permute-start.21 = (f32[192,256]{1,0:T(8,128)S(1)}, f32[192,256]{1,0:T(8,128)S(1)}, u32[]{:S(2)}, u32[]{:S(2)}) collective-permute-start(f32[192,256]{1,0:T(8,128)S(1)} %get-tuple-element.77.y1), channel_id=1, source_target_pairs={{0,1},{1,2},{2,3},{3,4},{4,5},{5,6},{6,7},{8,9},{9,10},{10,11},{11... | collective-permute-start | bytes 589832 | tf_op jit(solution)/shard_map/ppermute | solution.py:20
  224.9 6.4 %collective-permute-start.18 = (f32[192,256]{1,0:T(8,128)S(1)}, f32[192,256]{1,0:T(8,128)S(1)}, u32[]{:S(2)}, u32[]{:S(2)}) collective-permute-start(f32[192,256]{1,0:T(8,128)S(1)} %get-tuple-element.78.y2), channel_id=1, source_target_pairs={{8,0},{16,8},{24,16},{32,24},{40,32},{48,40},{56,48},{64,56},{72,6... | collective-permute-start | bytes 589832 | tf_op jit(solution)/shard_map/ppermute | solution.py:20
  228.1 7.9 %collective-permute-start.19 = (f32[192,256]{1,0:T(8,128)S(1)}, f32[192,256]{1,0:T(8,128)S(1)}, u32[]{:S(2)}, u32[]{:S(2)}) collective-permute-start(f32[192,256]{1,0:T(8,128)S(1)} %get-tuple-element.79.y3), channel_id=1, source_target_pairs={{1,0},{2,1},{3,2},{4,3},{5,4},{6,5},{7,6},{9,8},{10,9},{11,10},{12... | collective-permute-start | bytes 589832 | tf_op jit(solution)/shard_map/ppermute | solution.py:20
  239.1 69.1 %collective-permute-start.22 = (f32[192,256]{1,0:T(8,128)}, f32[192,256]{1,0:T(8,128)S(1)}, u32[]{:S(2)}, u32[]{:S(2)}) collective-permute-start(f32[192,256]{1,0:T(8,128)} %get-tuple-element.84), channel_id=1, source_target_pairs={{8,0},{16,8},{24,16},{32,24},{40,32},{48,40},{56,48},{64,56},{72,6... | collective-permute-start | bytes 589832 | tf_op jit(solution)/shard_map/ppermute | solution.py:20
  241.0 67.2 %collective-permute-start.23 = (f32[192,256]{1,0:T(8,128)S(1)}, f32[192,256]{1,0:T(8,128)S(1)}, u32[]{:S(2)}, u32[]{:S(2)}) collective-permute-start(f32[192,256]{1,0:T(8,128)S(1)} %get-tuple-element.85), channel_id=1, source_target_pairs={{1,0},{2,1},{3,2},{4,3},{5,4},{6,5},{7,6},{9,8},{10,9},{11,10},{12... | collective-permute-start | bytes 589832 | tf_op jit(solution)/shard_map/ppermute | solution.py:20
  308.2 1.1 copy-start.5
  309.3 1.0 copy-start.15
  (14 other events, 10.6 us)

commit v2 on v1

--- a/solution.py
+++ b/solution.py
@@ -54,7 +54,7 @@
     return jnp.sum(totals[0] - totals[1], axis=0, keepdims=True)
 
 
-def first_kernel(counts, matrix, gaps, below_wide, below_tile, res, gamma, f0, f1, f2, f3, lifted, product):
+def first_kernel(counts, matrix, gaps, below_wide, below_tile, res, gamma, f0, f1, f2, f3, lifted, product, behind):
     rows, columns = below_wide.shape
     for face in range(4):
         for piece in pieces(rows):
@@ -76,36 +76,52 @@
     return jnp.where(row_mask(piece.start, count, value.shape[1]), value, 0.0)
 
 
-def flex_kernel(counts, matrix, y0, y1, y2, y3, a0, a1, b0, b1, gamma, pre, sums, f0, f1, f2, f3, lifted, product):
+def flex_kernel(counts, matrix, y0, y1, y2, y3, a0, a1, b0, b1, gamma, pre, sums, f0, f1, f2, f3, lifted, product, behind):
     rows, columns = y0.shape
     own, across = (y0, y1, y2, y3), (a0, a1, b0, b1)
-    for face in range(4):
+
+    def place(face):
+        return (pre, face) if face < 2 else (behind, face - 2)
+
+    for face in range(4):
+        held, slot = place(face)
         for piece in pieces(rows):
             value = assembled(face, piece, own, across, counts[face])
-            pre[face, piece, :] = value
+            held[slot, piece, :] = value
             signed = value if face < 2 else -value
             lifted[face * rows + piece.start : face * rows + piece.stop, :] = signed.astype(BF16)
-    sums[0:1, :] = gamma[...]
-    sums[1:2, :] = multiply(matrix, lifted, lambda f, p: pre[f, p, :], (f0, f1, f2, f3), product)
-
-
-def step_sizes(first, sums, scal):
-    gamma, curvature = sums[0:1, :], sums[1:2, :]
-    if first:
+
+    def vector_at(face, piece):
+        held, slot = place(face)
+        return held[slot, piece, :]
+
+    curvature = multiply(matrix, lifted, vector_at, (f0, f1, f2, f3), product)
+    copies = sums.shape[0]
+    sums[:, 0:1, :] = jnp.broadcast_to(gamma[...][None], (copies, 1, columns))
+    sums[:, 1:2, :] = jnp.broadcast_to(curvature[None], (copies, 1, columns))
+
+
+def step_sizes(sums, scal):
+    gathered = jnp.sum(sums[...], axis=0)
+    gamma, curvature = gathered[0:1], gathered[1:2]
+    if scal is None:
         return gamma, gamma / curvature, None
     scaling = gamma / scal[0:1, :]
     return gamma, gamma / (curvature - scaling * gamma / scal[1:2, :]), scaling
 
 
 def update_kernel(first, *refs):
-    (counts, matrix, sums, y0, y1, y2, y3, a0, a1, b0, b1, pre, res), refs = refs[:13], refs[13:]
+    (counts, matrix, sums, y0, y1, y2, y3, a0, a1, b0, b1, res), refs = refs[:12], refs[12:]
+    scal = along = None
     if not first:
-        (scal, direction, along, mult), refs = refs[:4], refs[4:]
-    res_out, direction_out, along_out, mult_out, scal_out, gamma_out, f0, f1, f2, f3, lifted, product = refs
+        (scal, along), refs = refs[:2], refs[2:]
+    res_out, along_out, scal_out, gamma_out, f0, f1, f2, f3, lifted, product, behind = refs
     rows, columns = y0.shape
-    gamma, step, scaling = step_sizes(first, sums, None if first else scal)
+    gamma, step, scaling = step_sizes(sums, scal)
     scal_out[0:1, :] = gamma
     scal_out[1:2, :] = step
+    scal_out[2:3, :] = step if first else scal[1:2, :]
+    scal_out[3:4, :] = jnp.zeros_like(step) if first else scaling
     own, across = (y0, y1, y2, y3), (a0, a1, b0, b1)
     for face in range(4):
         for piece in pieces(rows):
@@ -117,26 +133,24 @@
             res_out[face, piece, :] = value
             signed = value if face < 2 else -value
             lifted[face * rows + piece.start : face * rows + piece.stop, :] = signed.astype(BF16)
-            if face < 2:
-                way = pre[face, piece, :]
-                if not first:
-                    way = way + scaling * direction[face, piece, :]
-                direction_out[face, piece, :] = way
-                moved = step * way
-                mult_out[face, piece, :] = moved if first else mult[face, piece, :] + moved
     gamma_out[...] = multiply(matrix, lifted, lambda f, p: res_out[f, p, :], (f0, f1, f2, f3), product)
 
 
-def last_kernel(counts, sums, y0, y1, a0, a1, pre, res, scal, direction, along, mult, mult_out, res_out):
+def last_kernel(counts, sums, y0, y1, a0, a1, res, scal, along, pre0, pre1, pre2, mult_out, res_out):
     rows, columns = y0.shape
-    gamma, step, scaling = step_sizes(False, sums, scal)
+    _, step2, scaling2 = step_sizes(sums, scal)
+    step1, step0, scaling1 = scal[1:2, :], scal[2:3, :], scal[3:4, :]
+    weight2 = step2
+    weight1 = step1 + step2 * scaling2
+    weight0 = step0 + weight1 * scaling1
     for face in range(2):
         for piece in pieces(rows):
             mapped = assembled(face, piece, (y0, y1), (a0, a1), counts[face])
-            mapped = mapped + scaling * along[face, piece, :]
-            res_out[face, piece, :] = res[face, piece, :] - step * mapped
-            way = pre[face, piece, :] + scaling * direction[face, piece, :]
-            mult_out[face, piece, :] = mult[face, piece, :] + step * way
+            mapped = mapped + scaling2 * along[face, piece, :]
+            res_out[face, piece, :] = res[face, piece, :] - step2 * mapped
+            mult_out[face, piece, :] = (
+                weight0 * pre0[face, piece, :] + weight1 * pre1[face, piece, :] + weight2 * pre2[face, piece, :]
+            )
 
 
 def call(kernel, outs, args, name, size=None):
@@ -145,6 +159,7 @@
     if size is not None:
         rows, columns = size
         scratch = [pltpu.VMEM((rows, columns), BF16), pltpu.VMEM((rows, columns), F32)]
+        scratch += [pltpu.VMEM((2, rows // 4, columns), F32)]
         flops = 2 * rows * rows * columns
     moved = sum(a.size * a.dtype.itemsize for a in args) + 4 * sum(o.size for o in outs)
     return pl.pallas_call(
@@ -159,16 +174,39 @@
     )(*args)
 
 
-def total(sums, stages):
-    for axes in stages:
-        sums = lax.optimization_barrier(lax.psum(sums, axes))
+def relay_kernel(held, out):
+    out[...] = jnp.broadcast_to(jnp.sum(held[...], axis=0, keepdims=True), out.shape)
+
+
+def split_kernel(gaps, wide, tile):
+    wide[...] = gaps[0]
+    tile[...] = gaps[1]
+
+
+def small_call(kernel, outs, arg, name):
+    return pl.pallas_call(
+        kernel,
+        out_shape=outs,
+        in_specs=[VMEM],
+        out_specs=[VMEM] * len(outs),
+        name=name,
+        compiler_params=pltpu.CompilerParams(vmem_limit_bytes=4 * 1024 * 1024),
+    )(arg)
+
+
+def gathered(sums, stages):
+    for index, axes in enumerate(stages):
+        if index:
+            out = jax.ShapeDtypeStruct((lax.axis_size(axes), *sums.shape[1:]), F32)
+            (sums,) = small_call(relay_kernel, [out], sums, "relay")
+        sums = lax.all_to_all(sums, axes, 0, 0)
     return sums
 
 
 STAGES = (
     ("y", "z", ("x", "core")),
-    ("y", "z", "x", "core"),
-    (("core", "y"), "x", "z"),
+    (("core", "y"), ("z", "x")),
+    (("x", "core", "y"), "z"),
 )
 
 
@@ -182,37 +220,41 @@
     two = jax.ShapeDtypeStruct((2, rows, columns), F32)
     face = jax.ShapeDtypeStruct((rows, columns), F32)
     line = jax.ShapeDtypeStruct((1, columns), F32)
-    pair = jax.ShapeDtypeStruct((2, columns), F32)
+    scalars = jax.ShapeDtypeStruct((4, columns), F32)
     faces = [face] * 4
 
-    below_tile = shifted(gaps[1], "y", 1)
-    below_wide = shifted(gaps[0], WIDE, 1)
+    wide_gaps, tile_gaps = small_call(split_kernel, [face, face], gaps, "split")
+    below_tile = shifted(tile_gaps, "y", 1)
+    below_wide = shifted(wide_gaps, WIDE, 1)
     res, gamma, *out = call(
         first_kernel, [four, line] + faces, [counts, schur, gaps, below_wide, below_tile], "first", size
     )
-    state = []
+    state, pres = [], []
     for iteration in range(ITERS):
+        stages = STAGES[iteration]
+        partial = jax.ShapeDtypeStruct((lax.axis_size(stages[0]), 2, columns), F32)
         across = exchange(out)
         pre, sums, *out = call(
-            flex_kernel, [four, pair] + faces, [counts, flex, *out, *across, gamma], "flex", size
+            flex_kernel, [two, partial] + faces, [counts, flex, *out, *across, gamma], "flex", size
         )
+        pres.append(pre)
         if iteration + 1 < ITERS:
             across = exchange(out)
-            sums = total(sums, STAGES[iteration])
-            res, direction, along, mult, scal, gamma, *out = call(
+            sums = gathered(sums, stages)
+            res, along, scal, gamma, *out = call(
                 functools.partial(update_kernel, iteration == 0),
-                [four, two, four, two, pair, line] + faces,
-                [counts, schur, sums, *out, *across, pre, res, *state],
+                [four, four, scalars, line] + faces,
+                [counts, schur, sums, *out, *across, res, *state],
                 "update",
                 size,
             )
-            state = [scal, direction, along, mult]
+            state = [scal, along]
         else:
             above_tile = shifted(out[3], "y", -1)
             above_wide = shifted(out[2], WIDE, -1)
-            sums = total(sums, STAGES[iteration])
+            sums = gathered(sums, stages)
             mult, res = call(
-                last_kernel, [two, two], [counts, sums, out[0], out[1], above_wide, above_tile, pre, res, *state], "last"
+                last_kernel, [two, two], [counts, sums, out[0], out[1], above_wide, above_tile, res, *state, *pres], "last"
             )
     return mult[None, None], res[None, None]
 

time: 315 us -> 233 us (0.74)
  blocking collectives: 189 us -> 64.9 us
  waiting for transfers between devices: 25.2 us -> 48.3 us
  starting transfers between devices: 59.5 us -> 82.1 us
    psum x10 -> x0, blocking collectives: 189 us -> none  [total(): sums = lax.optimization_barrier(lax.psum(sums, axes))]
    all_to_all x0 -> x4, blocking collectives: none -> 64.9 us  [gathered(): sums = lax.all_to_all(sums, axes, 0, 0)]
    all_to_all x0 -> x3, starting transfers between devices: none -> 24.6 us  [gathered(): sums = lax.all_to_all(sums, axes, 0, 0)]
    all_to_all x0 -> x3, waiting for transfers between devices: none -> 17.2 us  [gathered(): sums = lax.all_to_all(sums, axes, 0, 0)]
    ppermute x24, waiting for transfers between devices: 25.2 us -> 31 us  [shifted(): return lax.ppermute(block, axis, route)]
  transfers between devices with their start and end apart: 24 -> 27, of which waited for: 8 -> 14; matrix products, arithmetic and copies ran while one was open for 0% -> 0% of each run, Pallas kernels for 0% -> 0%
where the time goes in v2:
time: 233 us; the launch traced here: 231 us
  starting transfers between devices  82.1 us (35%)
  blocking collectives  64.9 us (28%)
  waiting for transfers between devices  48.3 us (21%)
  local copies, waits for them, and re-layouts  25.3 us (11%)
  Pallas kernels  9.61 us (4%)
    all_to_all x4, blocking collectives, gathered(): sums = lax.all_to_all(sums, axes, 0, 0)  64.9 us
    ppermute x24, starting transfers between devices, shifted(): return lax.ppermute(block, axis, route)  57.4 us
    ppermute x24, waiting for transfers between devices, shifted(): return lax.ppermute(block, axis, route)  31 us
    unnamed x76, local copies, waits for them, and re-layouts  25.3 us
    all_to_all x3, starting transfers between devices, gathered(): sums = lax.all_to_all(sums, axes, 0, 0)  24.6 us
    all_to_all x3, waiting for transfers between devices, gathered(): sums = lax.all_to_all(sums, axes, 0, 0)  17.2 us
    pallas_call x7, Pallas kernels, call(): pl.pallas_call(kernel, out_shape=outs, in_specs=[SMEM] + [VMEM] * (len(ar...  8.18 us
  transfers between devices with their start and end apart: 27, of which 14 were waited for; matrix products, arithmetic and copies ran while one was open for 0% of the time, Pallas kernels for 0%

profile of v2, /device:TPU:2, one launch (start us, length us, event | category | flops | bytes accessed | tf_op | source)
XLA Modules:
  0.0 231.2 jit_solution(15967865520629260289)
XLA Ops:
  1.7 2.1 collective-permute-start
  3.7 3.5 %collective-permute-start.1 = (f32[192,256]{1,0:T(8,128)S(1)}, f32[192,256]{1,0:T(8,128)S(1)}, u32[]{:S(2)}, u32[]{:S(2)}) collective-permute-start(f32[192,256]{1,0:T(8,128)S(1)} %get-tuple-element.47), channel_id=1, source_target_pairs={{0,1},{1,2},{2,3},{3,4},{4,5},{5,6},{6,7},{8,9},{9,10},{10,11},{11... | collective-permute-start | bytes 589832 | tf_op jit(solution)/shard_map/ppermute | solution.py:20
  7.2 1.6 collective-permute-done.below_wide
  8.8 3.1 %collective-permute-done.1.below_tile = f32[192,256]{1,0:T(8,128)S(1)} collective-permute-done((f32[192,256]{1,0:T(8,128)S(1)}, f32[192,256]{1,0:T(8,128)S(1)}, u32[]{:S(2)}, u32[]{:S(2)}) %collective-permute-start.1) | collective-permute-done | bytes 196640 | tf_op jit(solution)/shard_map/ppermute | solution.py:20
  11.9 1.3 copy-done.1
  15.8 2.7 %collective-permute-start.4 = (f32[192,256]{1,0:T(8,128)S(1)}, f32[192,256]{1,0:T(8,128)S(1)}, u32[]{:S(2)}, u32[]{:S(2)}) collective-permute-start(f32[192,256]{1,0:T(8,128)S(1)} %get-tuple-element.48.y0), channel_id=1, source_target_pairs={{0,8},{8,16},{16,24},{24,32},{32,40},{40,48},{48,56},{56,64},{64,7... | collective-permute-start | bytes 589832 | tf_op jit(solution)/shard_map/ppermute | solution.py:20
  18.5 4.1 %collective-permute-start.5 = (f32[192,256]{1,0:T(8,128)S(1)}, f32[192,256]{1,0:T(8,128)S(1)}, u32[]{:S(2)}, u32[]{:S(2)}) collective-permute-start(f32[192,256]{1,0:T(8,128)S(1)} %get-tuple-element.49.y1), channel_id=1, source_target_pairs={{0,1},{1,2},{2,3},{3,4},{4,5},{5,6},{6,7},{8,9},{9,10},{10,11},{11... | collective-permute-start | bytes 589832 | tf_op jit(solution)/shard_map/ppermute | solution.py:20
  22.6 2.9 %collective-permute-start.2 = (f32[192,256]{1,0:T(8,128)S(1)}, f32[192,256]{1,0:T(8,128)S(1)}, u32[]{:S(2)}, u32[]{:S(2)}) collective-permute-start(f32[192,256]{1,0:T(8,128)S(1)} %get-tuple-element.50.y2), channel_id=1, source_target_pairs={{8,0},{16,8},{24,16},{32,24},{40,32},{48,40},{56,48},{64,56},{72,6... | collective-permute-start | bytes 589832 | tf_op jit(solution)/shard_map/ppermute | solution.py:20
  25.6 1.3 collective-permute-start.3
  27.4 1.3 collective-permute-done.2.a0
  28.7 5.7 %collective-permute-done.3.a1 = f32[192,256]{1,0:T(8,128)S(1)} collective-permute-done((f32[192,256]{1,0:T(8,128)S(1)}, f32[192,256]{1,0:T(8,128)S(1)}, u32[]{:S(2)}, u32[]{:S(2)}) %collective-permute-start.3) | collective-permute-done | bytes 196640 | tf_op jit(solution)/shard_map/ppermute | solution.py:20
  35.5 1.9 collective-permute-start.8
  37.4 3.6 %collective-permute-start.9 = (f32[192,256]{1,0:T(8,128)S(1)}, f32[192,256]{1,0:T(8,128)S(1)}, u32[]{:S(2)}, u32[]{:S(2)}) collective-permute-start(f32[192,256]{1,0:T(8,128)S(1)} %get-tuple-element.55.refs_4_), channel_id=1, source_target_pairs={{0,1},{1,2},{2,3},{3,4},{4,5},{5,6},{6,7},{8,9},{9,10},{10,11},{11... | collective-permute-start | bytes 589832 | tf_op jit(solution)/shard_map/ppermute | solution.py:20
  41.1 3.4 %collective-permute-start.6 = (f32[192,256]{1,0:T(8,128)S(1)}, f32[192,256]{1,0:T(8,128)S(1)}, u32[]{:S(2)}, u32[]{:S(2)}) collective-permute-start(f32[192,256]{1,0:T(8,128)S(1)} %get-tuple-element.56.refs_5_), channel_id=1, source_target_pairs={{8,0},{16,8},{24,16},{32,24},{40,32},{48,40},{56,48},{64,56},{72,6... | collective-permute-start | bytes 589832 | tf_op jit(solution)/shard_map/ppermute | solution.py:20
  44.4 1.3 collective-permute-start.7
  45.7 17.9 %all_to_all.35.held = f32[8,2,256]{2,1,0:T(2,128)S(1)} all-to-all(f32[8,2,256]{2,1,0:T(2,128)S(1)} %get-tuple-element.53), channel_id=1, replica_groups=mesh['z'=12,'x'=4,'core'=2,'y'=8] {'y'}, dimensions={0} | all-to-all | bytes 32768 | tf_op jit(solution)/shard_map/all_to_all | solution.py:202
  63.7 25.4 %all_to_all.36.held = f32[12,2,256]{2,1,0:T(2,128)S(1)} all-to-all(f32[12,2,256]{2,1,0:T(2,128)S(1)} %relay.4), channel_id=1, replica_groups=mesh['z'=12,'x'=4,'core'=2,'y'=8] {'z'}, dimensions={0} | all-to-all | bytes 49152 | tf_op jit(solution)/shard_map/all_to_all | solution.py:202
  89.1 10.9 %all_to_all.37.refs_2_ = f32[8,2,256]{2,1,0:T(2,128)S(1)} all-to-all(f32[8,2,256]{2,1,0:T(2,128)S(1)} %relay.5), channel_id=1, replica_groups=mesh['z'=12,'x'=4,'core'=2,'y'=8] {'x','core'}, dimensions={0} | all-to-all | bytes 32768 | tf_op jit(solution)/shard_map/all_to_all | solution.py:202
  102.1 1.9 collective-permute-start.12
  104.1 2.5 %collective-permute-start.13 = (f32[192,256]{1,0:T(8,128)S(1)}, f32[192,256]{1,0:T(8,128)S(1)}, u32[]{:S(2)}, u32[]{:S(2)}) collective-permute-start(f32[192,256]{1,0:T(8,128)S(1)} %get-tuple-element.60.y1), channel_id=1, source_target_pairs={{0,1},{1,2},{2,3},{3,4},{4,5},{5,6},{6,7},{8,9},{9,10},{10,11},{11... | collective-permute-start | bytes 589832 | tf_op jit(solution)/shard_map/ppermute | solution.py:20
  106.6 3.4 %collective-permute-start.10 = (f32[192,256]{1,0:T(8,128)S(1)}, f32[192,256]{1,0:T(8,128)S(1)}, u32[]{:S(2)}, u32[]{:S(2)}) collective-permute-start(f32[192,256]{1,0:T(8,128)S(1)} %get-tuple-element.61.y2), channel_id=1, source_target_pairs={{8,0},{16,8},{24,16},{32,24},{40,32},{48,40},{56,48},{64,56},{72,6... | collective-permute-start | bytes 589832 | tf_op jit(solution)/shard_map/ppermute | solution.py:20
  110.0 1.3 collective-permute-start.11
  111.5 1.6 collective-permute-done.10.a0
  113.1 4.6 %collective-permute-done.11.a1 = f32[192,256]{1,0:T(8,128)S(1)} collective-permute-done((f32[192,256]{1,0:T(8,128)S(1)}, f32[192,256]{1,0:T(8,128)S(1)}, u32[]{:S(2)}, u32[]{:S(2)}) %collective-permute-start.11) | collective-permute-done | bytes 196640 | tf_op jit(solution)/shard_map/ppermute | solution.py:20
  120.2 10.6 %all_to_all.38.held = f32[16,2,256]{2,1,0:T(2,128)S(1)} all-to-all(f32[16,2,256]{2,1,0:T(2,128)S(1)} %get-tuple-element.64), channel_id=1, replica_groups=mesh['z'=12,'x'=4,'core'=2,'y'=8] {'core','y'}, dimensions={0} | all-to-all | bytes 65536 | tf_op jit(solution)/shard_map/all_to_all | solution.py:202
  131.6 7.1 %all-to-all-start.4 = ((f32[48,2,256]{2,1,0:T(2,128)}), f32[48,2,256]{2,1,0:T(2,128)S(1)}, u32[]{:S(2)}, u32[]{:S(2)}) async-start(f32[48,2,256]{2,1,0:T(2,128)} %relay.6), calls=%async_computation.4 | async-start | bytes 196608 | tf_op jit(solution)/shard_map/all_to_all | solution.py:202
  138.7 1.9 collective-permute-start.16
  140.6 2.7 %collective-permute-start.17 = (f32[192,256]{1,0:T(8,128)S(1)}, f32[192,256]{1,0:T(8,128)S(1)}, u32[]{:S(2)}, u32[]{:S(2)}) collective-permute-start(f32[192,256]{1,0:T(8,128)S(1)} %get-tuple-element.66.refs_4_), channel_id=1, source_target_pairs={{0,1},{1,2},{2,3},{3,4},{4,5},{5,6},{6,7},{8,9},{9,10},{10,11},{11... | collective-permute-start | bytes 589832 | tf_op jit(solution)/shard_map/ppermute | solution.py:20
  143.3 3.4 %collective-permute-start.14 = (f32[192,256]{1,0:T(8,128)S(1)}, f32[192,256]{1,0:T(8,128)S(1)}, u32[]{:S(2)}, u32[]{:S(2)}) collective-permute-start(f32[192,256]{1,0:T(8,128)S(1)} %get-tuple-element.67.refs_5_), channel_id=1, source_target_pairs={{8,0},{16,8},{24,16},{32,24},{40,32},{48,40},{56,48},{64,56},{72,6... | collective-permute-start | bytes 589832 | tf_op jit(solution)/shard_map/ppermute | solution.py:20
  147.4 1.3 collective-permute-start.15
  150.7 5.4 %collective-permute-done.15.refs_8_ = f32[192,256]{1,0:T(8,128)S(1)} collective-permute-done((f32[192,256]{1,0:T(8,128)}, f32[192,256]{1,0:T(8,128)S(1)}, u32[]{:S(2)}, u32[]{:S(2)}) %collective-permute-start.15) | collective-permute-done | bytes 196640 | tf_op jit(solution)/shard_map/ppermute | solution.py:20
  157.5 1.1 copy-done.8
  158.6 1.1 copy-done.10
  168.0 1.2 update.3
  169.2 1.9 collective-permute-start.20
  171.2 2.5 %collective-permute-start.21 = (f32[192,256]{1,0:T(8,128)S(1)}, f32[192,256]{1,0:T(8,128)S(1)}, u32[]{:S(2)}, u32[]{:S(2)}) collective-permute-start(f32[192,256]{1,0:T(8,128)S(1)} %get-tuple-element.73.y1), channel_id=1, source_target_pairs={{0,1},{1,2},{2,3},{3,4},{4,5},{5,6},{6,7},{8,9},{9,10},{10,11},{11... | collective-permute-start | bytes 589832 | tf_op jit(solution)/shard_map/ppermute | solution.py:20
  173.7 3.4 %collective-permute-start.18 = (f32[192,256]{1,0:T(8,128)S(1)}, f32[192,256]{1,0:T(8,128)S(1)}, u32[]{:S(2)}, u32[]{:S(2)}) collective-permute-start(f32[192,256]{1,0:T(8,128)S(1)} %get-tuple-element.74.y2), channel_id=1, source_target_pairs={{8,0},{16,8},{24,16},{32,24},{40,32},{48,40},{56,48},{64,56},{72,6... | collective-permute-start | bytes 589832 | tf_op jit(solution)/shard_map/ppermute | solution.py:20
  177.0 1.3 collective-permute-start.19
  178.6 1.6 collective-permute-done.18.a0
  180.2 5.1 %collective-permute-done.19.a1 = f32[192,256]{1,0:T(8,128)S(1)} collective-permute-done((f32[192,256]{1,0:T(8,128)S(1)}, f32[192,256]{1,0:T(8,128)S(1)}, u32[]{:S(2)}, u32[]{:S(2)}) %collective-permute-start.19) | collective-permute-done | bytes 196640 | tf_op jit(solution)/shard_map/ppermute | solution.py:20
  188.4 8.7 %all-to-all-start.5 = ((f32[64,2,256]{2,1,0:T(2,128)}), f32[64,2,256]{2,1,0:T(2,128)S(1)}, u32[]{:S(2)}, u32[]{:S(2)}) async-start(f32[64,2,256]{2,1,0:T(2,128)} %copy-done.31), calls=%async_computation.5 | async-start | bytes 262144 | tf_op jit(solution)/shard_map/all_to_all | solution.py:202
  197.1 2.0 collective-permute-start.22
  199.1 1.3 collective-permute-start.23
  200.4 6.8 %all-to-all-done.5.held = f32[64,2,256]{2,1,0:T(2,128)S(1)} async-done(((f32[64,2,256]{2,1,0:T(2,128)}), f32[64,2,256]{2,1,0:T(2,128)S(1)}, u32[]{:S(2)}, u32[]{:S(2)}) %all-to-all-start.5) | async-done | bytes 131104 | tf_op jit(solution)/shard_map/all_to_all | solution.py:202
  207.9 8.9 %all-to-all-start.6 = ((f32[12,2,256]{2,1,0:T(2,128)}), f32[12,2,256]{2,1,0:T(2,128)S(1)}, u32[]{:S(2)}, u32[]{:S(2)}) async-start(f32[12,2,256]{2,1,0:T(2,128)} %relay.7), calls=%async_computation.6 | async-start | bytes 49152 | tf_op jit(solution)/shard_map/all_to_all | solution.py:202
  216.8 10.4 %all-to-all-done.6.sums = f32[12,2,256]{2,1,0:T(2,128)S(1)} async-done(((f32[12,2,256]{2,1,0:T(2,128)}), f32[12,2,256]{2,1,0:T(2,128)S(1)}, u32[]{:S(2)}, u32[]{:S(2)}) %all-to-all-start.6) | async-done | bytes 24608 | tf_op jit(solution)/shard_map/all_to_all | solution.py:202
  227.8 1.1 copy-done.6
  229.7 1.6 last.1
  (98 shorter events, 28.6 us)
Async XLA Ops:
  0.6 33.8 %copy-start.35 = (s32[1,1,4]{2,1,0:T(1,128)S(1)}, s32[1,1,4]{2,1,0:T(1,128)}, u32[]{:S(2)}) copy-start(s32[1,1,4]{2,1,0:T(1,128)} %param.7) | copy-start | bytes 52
  0.6 1.0 copy-start.3
  1.6 32.8 %copy-start = (bf16[1,1,768,768]{3,2,1,0:T(8,128)(2,1)S(1)}, bf16[1,1,768,768]{3,2,1,0:T(8,128)(2,1)}, u32[]{:S(2)}) copy-start(bf16[1,1,768,768]{3,2,1,0:T(8,128)(2,1)} %param.5) | copy-start | bytes 3538948
  1.7 7.1 %collective-permute-start = (f32[192,256]{1,0:T(8,128)S(1)}, f32[192,256]{1,0:T(8,128)S(1)}, u32[]{:S(2)}, u32[]{:S(2)}) collective-permute-start(f32[192,256]{1,0:T(8,128)S(1)} %get-tuple-element.46), channel_id=1, source_target_pairs={{0,8},{8,16},{16,24},{24,32},{32,40},{40,48},{48,56},{56,64},{64,7... | collective-permute-start | bytes 589832 | tf_op jit(solution)/shard_map/ppermute | solution.py:20
  3.7 8.1 %collective-permute-start.1 = (f32[192,256]{1,0:T(8,128)S(1)}, f32[192,256]{1,0:T(8,128)S(1)}, u32[]{:S(2)}, u32[]{:S(2)}) collective-permute-start(f32[192,256]{1,0:T(8,128)S(1)} %get-tuple-element.47), channel_id=1, source_target_pairs={{0,1},{1,2},{2,3},{3,4},{4,5},{5,6},{6,7},{8,9},{9,10},{10,11},{11... | collective-permute-start | bytes 589832 | tf_op jit(solution)/shard_map/ppermute | solution.py:20
  11.9 1.3 copy-start.1
  13.1 1.0 copy-start.4
  15.8 11.0 %collective-permute-start.4 = (f32[192,256]{1,0:T(8,128)S(1)}, f32[192,256]{1,0:T(8,128)S(1)}, u32[]{:S(2)}, u32[]{:S(2)}) collective-permute-start(f32[192,256]{1,0:T(8,128)S(1)} %get-tuple-element.48.y0), channel_id=1, source_target_pairs={{0,8},{8,16},{16,24},{24,32},{32,40},{40,48},{48,56},{56,64},{64,7... | collective-permute-start | bytes 589832 | tf_op jit(solution)/shard_map/ppermute | solution.py:20
  18.5 8.9 %collective-permute-start.5 = (f32[192,256]{1,0:T(8,128)S(1)}, f32[192,256]{1,0:T(8,128)S(1)}, u32[]{:S(2)}, u32[]{:S(2)}) collective-permute-start(f32[192,256]{1,0:T(8,128)S(1)} %get-tuple-element.49.y1), channel_id=1, source_target_pairs={{0,1},{1,2},{2,3},{3,4},{4,5},{5,6},{6,7},{8,9},{9,10},{10,11},{11... | collective-permute-start | bytes 589832 | tf_op jit(solution)/shard_map/ppermute | solution.py:20
  22.6 6.1 %collective-permute-start.2 = (f32[192,256]{1,0:T(8,128)S(1)}, f32[192,256]{1,0:T(8,128)S(1)}, u32[]{:S(2)}, u32[]{:S(2)}) collective-permute-start(f32[192,256]{1,0:T(8,128)S(1)} %get-tuple-element.50.y2), channel_id=1, source_target_pairs={{8,0},{16,8},{24,16},{32,24},{40,32},{48,40},{56,48},{64,56},{72,6... | collective-permute-start | bytes 589832 | tf_op jit(solution)/shard_map/ppermute | solution.py:20
  25.6 8.9 %collective-permute-start.3 = (f32[192,256]{1,0:T(8,128)S(1)}, f32[192,256]{1,0:T(8,128)S(1)}, u32[]{:S(2)}, u32[]{:S(2)}) collective-permute-start(f32[192,256]{1,0:T(8,128)S(1)} %get-tuple-element.51.y3), channel_id=1, source_target_pairs={{1,0},{2,1},{3,2},{4,3},{5,4},{6,5},{7,6},{9,8},{10,9},{11,10},{12... | collective-permute-start | bytes 589832 | tf_op jit(solution)/shard_map/ppermute | solution.py:20
  34.4 65.6 %copy-start.2 = (bf16[1,1,768,768]{3,2,1,0:T(8,128)(2,1)S(1)}, bf16[1,1,768,768]{3,2,1,0:T(8,128)(2,1)}, u32[]{:S(2)}) copy-start(bf16[1,1,768,768]{3,2,1,0:T(8,128)(2,1)} %param.6) | copy-start | bytes 3538948
  35.5 64.5 %collective-permute-start.8 = (f32[192,256]{1,0:T(8,128)S(1)}, f32[192,256]{1,0:T(8,128)S(1)}, u32[]{:S(2)}, u32[]{:S(2)}) collective-permute-start(f32[192,256]{1,0:T(8,128)S(1)} %get-tuple-element.54.refs_3_), channel_id=1, source_target_pairs={{0,8},{8,16},{16,24},{24,32},{32,40},{40,48},{48,56},{56,64},{64,7... | collective-permute-start | bytes 589832 | tf_op jit(solution)/shard_map/ppermute | solution.py:20
  37.4 62.6 %collective-permute-start.9 = (f32[192,256]{1,0:T(8,128)S(1)}, f32[192,256]{1,0:T(8,128)S(1)}, u32[]{:S(2)}, u32[]{:S(2)}) collective-permute-start(f32[192,256]{1,0:T(8,128)S(1)} %get-tuple-element.55.refs_4_), channel_id=1, source_target_pairs={{0,1},{1,2},{2,3},{3,4},{4,5},{5,6},{6,7},{8,9},{9,10},{10,11},{11... | collective-permute-start | bytes 589832 | tf_op jit(solution)/shard_map/ppermute | solution.py:20
  41.1 59.0 %collective-permute-start.6 = (f32[192,256]{1,0:T(8,128)S(1)}, f32[192,256]{1,0:T(8,128)S(1)}, u32[]{:S(2)}, u32[]{:S(2)}) collective-permute-start(f32[192,256]{1,0:T(8,128)S(1)} %get-tuple-element.56.refs_5_), channel_id=1, source_target_pairs={{8,0},{16,8},{24,16},{32,24},{40,32},{48,40},{56,48},{64,56},{72,6... | collective-permute-start | bytes 589832 | tf_op jit(solution)/shard_map/ppermute | solution.py:20
  44.4 55.6 %collective-permute-start.7 = (f32[192,256]{1,0:T(8,128)S(1)}, f32[192,256]{1,0:T(8,128)S(1)}, u32[]{:S(2)}, u32[]{:S(2)}) collective-permute-start(f32[192,256]{1,0:T(8,128)S(1)} %get-tuple-element.57.refs_6_), channel_id=1, source_target_pairs={{1,0},{2,1},{3,2},{4,3},{5,4},{6,5},{7,6},{9,8},{10,9},{11,10},{12... | collective-permute-start | bytes 589832 | tf_op jit(solution)/shard_map/ppermute | solution.py:20
  101.2 0.9 copy-start.7
  102.1 16.7 %copy-start.9 = (f32[4,192,256]{2,1,0:T(8,128)}, f32[4,192,256]{2,1,0:T(8,128)S(1)}, u32[]{:S(2)}) copy-start(f32[4,192,256]{2,1,0:T(8,128)S(1)} %get-tuple-element.71.refs_13_) | copy-start | bytes 2359300
  102.1 9.1 %collective-permute-start.12 = (f32[192,256]{1,0:T(8,128)S(1)}, f32[192,256]{1,0:T(8,128)S(1)}, u32[]{:S(2)}, u32[]{:S(2)}) collective-permute-start(f32[192,256]{1,0:T(8,128)S(1)} %get-tuple-element.59.y0), channel_id=1, source_target_pairs={{0,8},{8,16},{16,24},{24,32},{32,40},{40,48},{48,56},{56,64},{64,7... | collective-permute-start | bytes 589832 | tf_op jit(solution)/shard_map/ppermute | solution.py:20
  104.1 7.5 %collective-permute-start.13 = (f32[192,256]{1,0:T(8,128)S(1)}, f32[192,256]{1,0:T(8,128)S(1)}, u32[]{:S(2)}, u32[]{:S(2)}) collective-permute-start(f32[192,256]{1,0:T(8,128)S(1)} %get-tuple-element.60.y1), channel_id=1, source_target_pairs={{0,1},{1,2},{2,3},{3,4},{4,5},{5,6},{6,7},{8,9},{9,10},{10,11},{11... | collective-permute-start | bytes 589832 | tf_op jit(solution)/shard_map/ppermute | solution.py:20
  106.6 6.5 %collective-permute-start.10 = (f32[192,256]{1,0:T(8,128)S(1)}, f32[192,256]{1,0:T(8,128)S(1)}, u32[]{:S(2)}, u32[]{:S(2)}) collective-permute-start(f32[192,256]{1,0:T(8,128)S(1)} %get-tuple-element.61.y2), channel_id=1, source_target_pairs={{8,0},{16,8},{24,16},{32,24},{40,32},{48,40},{56,48},{64,56},{72,6... | collective-permute-start | bytes 589832 | tf_op jit(solution)/shard_map/ppermute | solution.py:20
  110.0 7.8 %collective-permute-start.11 = (f32[192,256]{1,0:T(8,128)S(1)}, f32[192,256]{1,0:T(8,128)S(1)}, u32[]{:S(2)}, u32[]{:S(2)}) collective-permute-start(f32[192,256]{1,0:T(8,128)S(1)} %get-tuple-element.62.y3), channel_id=1, source_target_pairs={{1,0},{2,1},{3,2},{4,3},{5,4},{6,5},{7,6},{9,8},{10,9},{11,10},{12... | collective-permute-start | bytes 589832 | tf_op jit(solution)/shard_map/ppermute | solution.py:20
  120.2 37.2 %copy-start.15 = (f32[192,256]{1,0:T(8,128)}, f32[192,256]{1,0:T(8,128)S(1)}, u32[]{:S(2)}) copy-start(f32[192,256]{1,0:T(8,128)S(1)} %get-tuple-element.65.refs_3_) | copy-start | bytes 589828
  120.2 37.2 %copy-start.17 = (f32[192,256]{1,0:T(8,128)}, f32[192,256]{1,0:T(8,128)S(1)}, u32[]{:S(2)}) copy-start(f32[192,256]{1,0:T(8,128)S(1)} %get-tuple-element.66.refs_4_) | copy-start | bytes 589828
  131.6 25.2 %all-to-all-start.4 = ((f32[48,2,256]{2,1,0:T(2,128)}), f32[48,2,256]{2,1,0:T(2,128)S(1)}, u32[]{:S(2)}, u32[]{:S(2)}) async-start(f32[48,2,256]{2,1,0:T(2,128)} %relay.6), calls=%async_computation.4 | async-start | bytes 196608 | tf_op jit(solution)/shard_map/all_to_all | solution.py:202
  138.7 10.0 %collective-permute-start.16 = (f32[192,256]{1,0:T(8,128)S(1)}, f32[192,256]{1,0:T(8,128)S(1)}, u32[]{:S(2)}, u32[]{:S(2)}) collective-permute-start(f32[192,256]{1,0:T(8,128)S(1)} %get-tuple-element.65.refs_3_), channel_id=1, source_target_pairs={{0,8},{8,16},{16,24},{24,32},{32,40},{40,48},{48,56},{56,64},{64,7... | collective-permute-start | bytes 589832 | tf_op jit(solution)/shard_map/ppermute | solution.py:20
  140.6 8.7 %collective-permute-start.17 = (f32[192,256]{1,0:T(8,128)S(1)}, f32[192,256]{1,0:T(8,128)S(1)}, u32[]{:S(2)}, u32[]{:S(2)}) collective-permute-start(f32[192,256]{1,0:T(8,128)S(1)} %get-tuple-element.66.refs_4_), channel_id=1, source_target_pairs={{0,1},{1,2},{2,3},{3,4},{4,5},{5,6},{6,7},{8,9},{9,10},{10,11},{11... | collective-permute-start | bytes 589832 | tf_op jit(solution)/shard_map/ppermute | solution.py:20
  143.3 6.7 %collective-permute-start.14 = (f32[192,256]{1,0:T(8,128)S(1)}, f32[192,256]{1,0:T(8,128)S(1)}, u32[]{:S(2)}, u32[]{:S(2)}) collective-permute-start(f32[192,256]{1,0:T(8,128)S(1)} %get-tuple-element.67.refs_5_), channel_id=1, source_target_pairs={{8,0},{16,8},{24,16},{32,24},{40,32},{48,40},{56,48},{64,56},{72,6... | collective-permute-start | bytes 589832 | tf_op jit(solution)/shard_map/ppermute | solution.py:20
  147.4 8.7 %collective-permute-start.15 = (f32[192,256]{1,0:T(8,128)}, f32[192,256]{1,0:T(8,128)S(1)}, u32[]{:S(2)}, u32[]{:S(2)}) collective-permute-start(f32[192,256]{1,0:T(8,128)} %copy-done.21), channel_id=1, source_target_pairs={{1,0},{2,1},{3,2},{4,3},{5,4},{6,5},{7,6},{9,8},{10,9},{11,10},{12... | collective-permute-start | bytes 589832 | tf_op jit(solution)/shard_map/ppermute | solution.py:20
  157.5 1.1 copy-start.8
  158.6 1.1 copy-start.10
  160.6 0.9 copy-start.16
  161.5 0.9 copy-start.18
  162.5 0.9 copy-start.20
  163.4 0.9 copy-start.22
  164.3 0.9 copy-start.24
  166.2 0.9 copy-start.28
  169.2 17.2 %copy-start.5 = (f32[4,192,256]{2,1,0:T(8,128)}, f32[4,192,256]{2,1,0:T(8,128)S(1)}, u32[]{:S(2)}) copy-start(f32[4,192,256]{2,1,0:T(8,128)S(1)} %get-tuple-element.84.along) | copy-start | bytes 2359300
  169.2 9.1 %collective-permute-start.20 = (f32[192,256]{1,0:T(8,128)S(1)}, f32[192,256]{1,0:T(8,128)S(1)}, u32[]{:S(2)}, u32[]{:S(2)}) collective-permute-start(f32[192,256]{1,0:T(8,128)S(1)} %get-tuple-element.72.y0), channel_id=1, source_target_pairs={{0,8},{8,16},{16,24},{24,32},{32,40},{40,48},{48,56},{56,64},{64,7... | collective-permute-start | bytes 589832 | tf_op jit(solution)/shard_map/ppermute | solution.py:20
  171.2 7.5 %collective-permute-start.21 = (f32[192,256]{1,0:T(8,128)S(1)}, f32[192,256]{1,0:T(8,128)S(1)}, u32[]{:S(2)}, u32[]{:S(2)}) collective-permute-start(f32[192,256]{1,0:T(8,128)S(1)} %get-tuple-element.73.y1), channel_id=1, source_target_pairs={{0,1},{1,2},{2,3},{3,4},{4,5},{5,6},{6,7},{8,9},{9,10},{10,11},{11... | collective-permute-start | bytes 589832 | tf_op jit(solution)/shard_map/ppermute | solution.py:20
  173.7 6.5 %collective-permute-start.18 = (f32[192,256]{1,0:T(8,128)S(1)}, f32[192,256]{1,0:T(8,128)S(1)}, u32[]{:S(2)}, u32[]{:S(2)}) collective-permute-start(f32[192,256]{1,0:T(8,128)S(1)} %get-tuple-element.74.y2), channel_id=1, source_target_pairs={{8,0},{16,8},{24,16},{32,24},{40,32},{48,40},{56,48},{64,56},{72,6... | collective-permute-start | bytes 589832 | tf_op jit(solution)/shard_map/ppermute | solution.py:20
  177.0 8.3 %collective-permute-start.19 = (f32[192,256]{1,0:T(8,128)S(1)}, f32[192,256]{1,0:T(8,128)S(1)}, u32[]{:S(2)}, u32[]{:S(2)}) collective-permute-start(f32[192,256]{1,0:T(8,128)S(1)} %get-tuple-element.75.y3), channel_id=1, source_target_pairs={{1,0},{2,1},{3,2},{4,3},{5,4},{6,5},{7,6},{9,8},{10,9},{11,10},{12... | collective-permute-start | bytes 589832 | tf_op jit(solution)/shard_map/ppermute | solution.py:20
  185.3 42.5 %copy-start.12 = (f32[2,192,256]{2,1,0:T(8,128)S(1)}, f32[2,192,256]{2,1,0:T(8,128)}, u32[]{:S(2)}) copy-start(f32[2,192,256]{2,1,0:T(8,128)} %copy-done.11) | copy-start | bytes 1179652
  188.4 18.8 %all-to-all-start.5 = ((f32[64,2,256]{2,1,0:T(2,128)}), f32[64,2,256]{2,1,0:T(2,128)S(1)}, u32[]{:S(2)}, u32[]{:S(2)}) async-start(f32[64,2,256]{2,1,0:T(2,128)} %copy-done.31), calls=%async_computation.5 | async-start | bytes 262144 | tf_op jit(solution)/shard_map/all_to_all | solution.py:202
  197.1 19.7 %collective-permute-start.22 = (f32[192,256]{1,0:T(8,128)}, f32[192,256]{1,0:T(8,128)S(1)}, u32[]{:S(2)}, u32[]{:S(2)}) collective-permute-start(f32[192,256]{1,0:T(8,128)} %copy-done.37), channel_id=1, source_target_pairs={{8,0},{16,8},{24,16},{32,24},{40,32},{48,40},{56,48},{64,56},{72,6... | collective-permute-start | bytes 589832 | tf_op jit(solution)/shard_map/ppermute | solution.py:20
  199.1 17.7 %collective-permute-start.23 = (f32[192,256]{1,0:T(8,128)}, f32[192,256]{1,0:T(8,128)S(1)}, u32[]{:S(2)}, u32[]{:S(2)}) collective-permute-start(f32[192,256]{1,0:T(8,128)} %copy-done.36), channel_id=1, source_target_pairs={{1,0},{2,1},{3,2},{4,3},{5,4},{6,5},{7,6},{9,8},{10,9},{11,10},{12... | collective-permute-start | bytes 589832 | tf_op jit(solution)/shard_map/ppermute | solution.py:20
  207.9 19.3 %all-to-all-start.6 = ((f32[12,2,256]{2,1,0:T(2,128)}), f32[12,2,256]{2,1,0:T(2,128)S(1)}, u32[]{:S(2)}, u32[]{:S(2)}) async-start(f32[12,2,256]{2,1,0:T(2,128)} %relay.7), calls=%async_computation.6 | async-start | bytes 49152 | tf_op jit(solution)/shard_map/all_to_all | solution.py:202
  227.8 1.1 copy-start.6
  (17 other events, 12.2 us)
